TPU v7x, 32 devices: a whole 2x2x4 slice. The times are simulated.
32 devices in a mesh: groups: 2 (over x), row: 16 (over z, y, core).
Axes of the slice: x: 2, y: 2, z: 4, core: 2. Of those that a mesh axis runs over, the one named last changes fastest.
Arguments:
- factor_b: bfloat16 [64, 131072], P(None, ('groups', 'row')), parts along dimension 1, may hold values from -12 to 12
- factor_c: bfloat16 [64, 131072], P(None, ('groups', 'row')), parts along dimension 1, may hold values from -12 to 12
- sample_j: int32 [262144], P(('groups', 'row')), parts along dimension 0, may hold values from 0 to 65535, as said below
- sample_k: int32 [16, 32, 512], P(None, ('groups', 'row')), parts along dimension 1, may hold values from 0 to 65535, as said below
- sample_weight: float32 [262144], P(('groups', 'row')), parts along dimension 0, may hold values from 0.5 to 3.5
- block_values: bfloat16 [32, 16, 4, 4, 128], P(('groups', 'row')), parts along dimension 0, may hold values from -24 to 24
- block_sample: int32 [32, 16, 4, 4], P(('groups', 'row')), parts along dimension 0, may hold values from 0 to 8191
- block_count: int32 [32, 16, 4, 4], P(('groups', 'row')), parts along dimension 0, may hold values from 0 to 128, as said below
Outputs:
- factor_new: bfloat16 [64, 16384], P(None, ('groups', 'row')), parts along dimension 1
- scales: float32 [128], P('groups'), parts along dimension 0
There are 2 independent parts, one for each index of `groups`. A program takes and returns all parts, laid end to end along the dimension named above; each array names one. Nothing has to cross between parts.
Inputs may be any that keep to these rules, and one draw needn't show every extreme that they name: sample_j[s] lies in rows s // 8192 * 4096 to s // 8192 * 4096 + 4095. sample_k[d, e, i] is the third-mode index of sample d * 8192 + e * 512 + i and lies in rows e * 4096 to e * 4096 + 4095. `block_count`: 0 marks an empty slot; slot [p, p, 0, 0] holds 128 for every p.
All inputs are finite; a program needn't handle non-finite values.
Results may differ from a plain program's by a relative error of at most 0.0051.
Values may be sent and summed in bfloat16 or wider, within the bound.
A program may use at most 64 MiB of HBM per device.

v0:
```python
import functools

import jax
import jax.numpy as jnp
from jax import lax
from jax.experimental import pallas as pl
from jax.experimental.pallas import tpu as pltpu
from jax.sharding import PartitionSpec as P

NT = (((1,), (1,)), ((), ()))
TN = (((0,), (0,)), ((), ()))
MESH = pl.DeviceIdType.MESH


def fold_table(table_ref, folded, width):
    rank = table_ref.shape[0]
    for part in range(table_ref.shape[1] // width):
        folded[part * rank : (part + 1) * rank, :] = table_ref[
            :, part * width : (part + 1) * width
        ]


def pick_columns(folded, index, rank):
    width = folded.shape[1]
    count = index.shape[1]
    low = lax.rem(index, width)
    high = lax.div(index, width)
    rows = lax.broadcasted_iota(jnp.int16, (width, count), 0)
    one_hot = jnp.where(rows == low.astype(jnp.int16), jnp.bfloat16(1), jnp.bfloat16(0))
    products = jnp.dot(folded[...], one_hot, preferred_element_type=jnp.float32)
    picked = products[:rank]
    high = jnp.broadcast_to(high, (rank, count))
    for part in range(1, folded.shape[0] // rank):
        picked = jnp.where(high == part, products[part * rank : (part + 1) * rank], picked)
    return picked


def partner(me, mask, n):
    other, bit = 0, 1
    while bit < n:
        other = other + bit * lax.rem(lax.div(me, bit) + lax.div(mask, bit), 2)
        bit *= 2
    return other


def block_column(table_ref):
    table = jnp.concatenate([table_ref[tile] for tile in range(table_ref.shape[0])], axis=0)
    return jnp.concatenate(
        [table[:, peer : peer + 1] for peer in range(table.shape[1])], axis=0
    )


def inverse(matrix):
    order = matrix.shape[0]
    lanes = lax.broadcasted_iota(jnp.int32, (1, order), 1)
    rows = lax.broadcasted_iota(jnp.int32, (order, 1), 0)
    for k in range(order):
        row = matrix[k : k + 1, :]
        column = matrix[:, k : k + 1]
        pivot = 1.0 / row[:, k : k + 1]
        scaled = jnp.where(lanes == k, 1.0, row) * pivot
        matrix = jnp.where(
            rows == k, scaled, jnp.where(lanes == k, 0.0, matrix) - column * scaled
        )
    return matrix


def kernel(
    n,
    tiles,
    slots,
    width,
    total_rows,
    total_samples,
    b_ref,
    c_ref,
    j_ref,
    k_ref,
    w_ref,
    values_ref,
    sample_ref,
    count_ref,
    out_ref,
    scales_ref,
    folded_b,
    folded_c,
    c_out,
    c_in,
    b_weighted,
    values_out,
    values_in,
    picks_out,
    picks_in,
    gram_out,
    gram_in,
    share_out,
    share_in,
    sample_column,
    sums_out,
    sums_in,
    c_send,
    c_recv,
    values_send,
    values_recv,
    picks_send,
    picks_recv,
    gram_send,
    gram_recv,
    share_send,
    share_recv,
    sums_send,
    sums_recv,
):
    me = lax.axis_index("row")
    rank, b_rows = b_ref.shape
    c_rows = c_ref.shape[1]
    share = rank // n
    per_peer = tiles * slots
    blocks = n * per_peer
    chunk = c_in.shape[2]

    def each_peer(body):
        def step(turn, carry):
            body(partner(me, n - turn, n))
            return carry

        lax.fori_loop(1, n, step, 0)

    def copy_to(peer, source, target, send, recv):
        return pltpu.make_async_remote_copy(
            src_ref=source,
            dst_ref=target.at[me],
            send_sem=send.at[peer],
            recv_sem=recv.at[me],
            device_id={"row": peer},
            device_id_type=MESH,
        )

    def copy_from(peer, source, target, send, recv):
        return pltpu.make_async_remote_copy(
            src_ref=source,
            dst_ref=target.at[peer],
            send_sem=send.at[peer],
            recv_sem=recv.at[peer],
            device_id={"row": peer},
            device_id_type=MESH,
        )

    barrier = pltpu.get_barrier_semaphore()
    each_peer(
        lambda peer: pl.semaphore_signal(
            barrier, inc=1, device_id={"row": peer}, device_id_type=MESH
        )
    )
    fold_table(c_ref, folded_c, width)
    fold_table(b_ref, folded_b, width)
    lanes = lax.broadcasted_iota(jnp.int32, (blocks, 128), 1)
    counts = block_column(count_ref)
    live = lanes < counts
    masked = jnp.where(live, values_ref[...].astype(jnp.float32), 0.0).astype(jnp.bfloat16)
    values_out[...] = masked.reshape(values_out.shape)
    values_in[me] = values_out[me]
    c_in[me] = pick_columns(folded_c, k_ref[me] - me * c_rows, rank).astype(jnp.bfloat16)
    pl.semaphore_wait(barrier, n - 1)

    def send_c(peer):
        c_out[peer] = pick_columns(folded_c, k_ref[peer] - me * c_rows, rank).astype(
            jnp.bfloat16
        )
        copy_to(peer, c_out.at[peer], c_in, c_send, c_recv).start()

    each_peer(send_c)
    each_peer(
        lambda peer: copy_to(
            peer, values_out.at[peer], values_in, values_send, values_recv
        ).start()
    )

    def pick_b(part, carry):
        picked = pick_columns(folded_b, j_ref[part] - me * b_rows, rank)
        b_weighted[part] = w_ref[part] * picked
        return carry

    lax.fori_loop(0, n, pick_b, 0)

    columns = lax.broadcasted_iota(jnp.int32, (blocks, chunk), 1)
    sample_column[...] = block_column(sample_ref)
    counts = block_column(count_ref)

    def add_chunk(part, carry):
        gram, picks = carry
        weights = w_ref[part]
        sketch = b_weighted[part] * c_in[part].astype(jnp.float32)
        top = sketch.astype(jnp.bfloat16)
        rest = (sketch - top.astype(jnp.float32)).astype(jnp.bfloat16)
        both = jnp.concatenate([top, rest], axis=0)
        gram = gram + lax.dot_general(both, both, NT, preferred_element_type=jnp.float32)
        weighted = (weights * sketch).astype(jnp.bfloat16)
        chosen = columns == sample_column[...] - part * chunk
        chosen = jnp.where(chosen, 1.0, 0.0).astype(jnp.bfloat16)
        picks = picks + lax.dot_general(
            chosen, weighted, NT, preferred_element_type=jnp.float32
        )
        return gram, picks

    def add_peer(turn, carry):
        part = partner(me, n - turn, n)
        copy_from(part, c_out.at[part], c_in, c_send, c_recv).wait_recv()
        return add_chunk(part, carry)

    carry = (
        jnp.zeros((2 * rank, 2 * rank), jnp.float32),
        jnp.zeros((blocks, rank), jnp.float32),
    )
    carry = add_chunk(me, carry)
    gram, picks = lax.fori_loop(1, n, add_peer, carry)

    gram = gram[:rank, :rank] + gram[:rank, rank:] + gram[rank:, :rank] + gram[rank:, rank:]
    live_local = jnp.sum(counts.astype(jnp.float32), axis=0, keepdims=True)
    gram = jnp.concatenate([gram, jnp.broadcast_to(live_local, gram.shape)], axis=1)
    gram_out[...] = jnp.zeros_like(gram_out)
    for part in range(n):
        gram_out[part, :share, :] = gram[part * share : (part + 1) * share]
    gram_in[me] = gram_out[me]
    picks = jnp.concatenate([picks, jnp.zeros_like(picks)], axis=1).astype(jnp.bfloat16)
    picks_out[...] = picks.reshape(picks_out.shape)
    picks_in[me] = picks_out[me]

    def send_sums(peer):
        copy_to(peer, gram_out.at[peer], gram_in, gram_send, gram_recv).start()
        copy_to(peer, picks_out.at[peer], picks_in, picks_send, picks_recv).start()

    each_peer(send_sums)

    def receive_sums(peer):
        copy_from(peer, gram_out.at[peer], gram_in, gram_send, gram_recv).wait_recv()

    each_peer(receive_sums)
    share_out[...] = lax.fori_loop(
        1, n, lambda part, carry: carry + gram_in[part], gram_in[0]
    )
    share_in[me] = share_out[...]
    each_peer(
        lambda peer: copy_to(peer, share_out, share_in, share_send, share_recv).start()
    )

    def receive_blocks(peer):
        copy_from(
            peer, values_out.at[peer], values_in, values_send, values_recv
        ).wait_recv()
        copy_from(peer, picks_out.at[peer], picks_in, picks_send, picks_recv).wait_recv()

    each_peer(receive_blocks)
    arrived = values_in[...].reshape(blocks, 128).astype(jnp.float32)
    block_rows = lax.broadcasted_iota(jnp.int32, (blocks, 128), 0)
    tile_of = lax.rem(lax.div(block_rows, slots), tiles)
    spread = jnp.concatenate(
        [jnp.where(tile_of == tile, arrived, 0.0) for tile in range(tiles)], axis=1
    ).astype(jnp.bfloat16)
    gathered = lax.dot_general(
        picks_in[...].reshape(blocks, 2 * rank), spread, TN, preferred_element_type=jnp.float32
    )[:rank]
    each_peer(
        lambda peer: copy_from(peer, share_out, share_in, share_send, share_recv).wait_recv()
    )
    total = jnp.concatenate([share_in[part][:share] for part in range(n)], axis=0)
    ridge = 0.05 * total[:1, rank:] / total_rows
    gram_rows = lax.broadcasted_iota(jnp.int32, (rank, rank), 0)
    diagonal = gram_rows == lax.broadcasted_iota(jnp.int32, (rank, rank), 1)
    system = total[:, :rank] / total_samples + jnp.where(diagonal, ridge, 0.0)
    inverted = inverse(system)
    update = jnp.dot(
        inverted,
        gathered,
        precision=lax.Precision.HIGHEST,
        preferred_element_type=jnp.float32,
    )
    squares = jnp.sum(update * update, axis=1, keepdims=True)
    squares = jnp.sum(jnp.where(diagonal, squares, 0.0), axis=0, keepdims=True)
    squares = jnp.concatenate([squares, jnp.zeros_like(squares)], axis=1)
    sums_out[...] = jnp.broadcast_to(squares, sums_out.shape)
    sums_in[me] = sums_out[...]
    each_peer(
        lambda peer: copy_to(peer, sums_out, sums_in, sums_send, sums_recv).start()
    )
    each_peer(
        lambda peer: copy_from(peer, sums_out, sums_in, sums_send, sums_recv).wait_recv()
    )
    sums = lax.fori_loop(1, n, lambda part, carry: carry + sums_in[part], sums_in[0])
    scales = jnp.sqrt(sums[:1, :rank] / total_rows + 1e-06)
    scales_ref[...] = scales
    scale_column = jnp.sum(jnp.where(diagonal, scales, 0.0), axis=1, keepdims=True)
    out_ref[...] = (update / scale_column).astype(out_ref.dtype)

    def finish(peer):
        copy_to(peer, c_out.at[peer], c_in, c_send, c_recv).wait_send()
        copy_to(peer, values_out.at[peer], values_in, values_send, values_recv).wait_send()
        copy_to(peer, gram_out.at[peer], gram_in, gram_send, gram_recv).wait_send()
        copy_to(peer, share_out, share_in, share_send, share_recv).wait_send()
        copy_to(peer, picks_out.at[peer], picks_in, picks_send, picks_recv).wait_send()
        copy_to(peer, sums_out, sums_in, sums_send, sums_recv).wait_send()

    each_peer(finish)


def shards(
    factor_b, factor_c, sample_j, sample_k, sample_weight, block_values, block_sample, block_count
):
    rank, b_rows = factor_b.shape
    n, _, chunk = sample_k.shape
    _, _, tiles, slots, tile_rows = block_values.shape
    samples = sample_j.shape[0]
    per_peer = tiles * slots
    blocks = n * per_peer
    width = 512
    bf16, f32 = jnp.bfloat16, jnp.float32
    vmem = pl.BlockSpec(memory_space=pltpu.VMEM)
    factor_new, scales = pl.pallas_call(
        functools.partial(
            kernel, n, tiles, slots, width, tiles * tile_rows * n, samples * n
        ),
        out_shape=(
            jax.ShapeDtypeStruct((rank, tiles * tile_rows), bf16),
            jax.ShapeDtypeStruct((1, rank), f32),
        ),
        in_specs=[vmem] * 8,
        out_specs=(vmem, vmem),
        scratch_shapes=[
            pltpu.VMEM((b_rows // width * rank, width), bf16),
            pltpu.VMEM((factor_c.shape[1] // width * rank, width), bf16),
            pltpu.VMEM((n, rank, chunk), bf16),
            pltpu.VMEM((n, rank, chunk), bf16),
            pltpu.VMEM((n, rank, chunk), f32),
            pltpu.VMEM((n, per_peer, tile_rows), bf16),
            pltpu.VMEM((n, per_peer, tile_rows), bf16),
            pltpu.VMEM((n, per_peer, 2 * rank), bf16),
            pltpu.VMEM((n, per_peer, 2 * rank), bf16),
            pltpu.VMEM((n, 8, 2 * rank), f32),
            pltpu.VMEM((n, 8, 2 * rank), f32),
            pltpu.VMEM((8, 2 * rank), f32),
            pltpu.VMEM((n, 8, 2 * rank), f32),
            pltpu.VMEM((blocks, 1), jnp.int32),
            pltpu.VMEM((8, 2 * rank), f32),
            pltpu.VMEM((n, 8, 2 * rank), f32),
        ]
        + [pltpu.SemaphoreType.DMA((n,))] * 12,
        compiler_params=pltpu.CompilerParams(collective_id=0, has_side_effects=True),
    )(
        factor_b,
        factor_c,
        sample_j.reshape(n, 1, chunk),
        sample_k,
        sample_weight.reshape(n, 1, chunk),
        block_values.reshape(blocks, tile_rows),
        block_sample[0].transpose(1, 2, 0),
        block_count[0].transpose(1, 2, 0),
    )
    return factor_new, scales.reshape(rank)


def solution(mesh):
    in_specs = (
        P(None, ("groups", "row")),
        P(None, ("groups", "row")),
        P(("groups", "row")),
        P(None, ("groups", "row"), None),
        P(("groups", "row")),
        P(("groups", "row"), None, None, None, None),
        P(("groups", "row"), None, None, None),
        P(("groups", "row"), None, None, None),
    )
    out_specs = (P(None, ("groups", "row")), P("groups"))
    return jax.shard_map(shards, mesh=mesh, in_specs=in_specs, out_specs=out_specs, check_vma=False)
```

profile of v0, /device:TPU:0, one launch (start us, length us, event | category | flops | bytes accessed | tf_op | source)
XLA Modules:
  0.0 59.5 jit_solution(15553964342946624761)
XLA Ops:
  0.6 56.9 %shard_map.95 = (bf16[64,512]{1,0:T(8,128)(2,1)}, f32[1,64]{1,0:T(1,128)}) custom-call(bf16[64,4096]{1,0:T(8,128)(2,1)} %b_ref.1, bf16[64,4096]{1,0:T(8,128)(2,1)} %c_ref.1, s32[16,1,512]{2,1,0:T(1,128)} %bitcast.11, s32[16,1,512]{2,1,0:T(1,128)} %k_ref.1, f32[16,1,512]{2,1,0:T(1,128)} %bitcast.12, bf16[256,128]{1,0:T(8,128)(2,1)} %bitcast.10, ...), custom_call_target="tpu_custom_call" | custom-call | tf_op jit(solution)/shard_map/pallas_call | solution.py:318
  57.5 0.0 copy-start
  57.5 1.5 %copy.12 = bf16[64,512]{1,0:T(8,128)(2,1)} copy(bf16[64,512]{1,0:T(8,128)(2,1)} %get-tuple-element.8) | data formatting | bytes 131072
  59.0 0.0 copy-done
  59.0 0.5 copy.13
Async XLA Ops:
  57.5 1.5 %copy-start = (f32[1,64]{1,0:T(1,128)S(1)}, f32[1,64]{1,0:T(1,128)}, u32[]{:S(2)}) copy-start(f32[1,64]{1,0:T(1,128)} %get-tuple-element.5) | copy-start | bytes 772
where the time goes:
time: 59.7 us; the launch traced here: 59.5 us
  Pallas kernels  56.9 us (95%)
  local copies, waits for them, and re-layouts  1.99 us (3%)
  between operations  0.65 us (1%)
    pallas_call x1, Pallas kernels, shards(): pl.pallas_call(functools.partial(kernel, n, tiles, slots, width, tiles *...  56.9 us
    unnamed x4, local copies, waits for them, and re-layouts  1.99 us

commit v1 on v0

v1 whole, which is shorter than its diff:
```python
import functools

import jax
import jax.numpy as jnp
from jax import lax
from jax.experimental import pallas as pl
from jax.experimental.pallas import tpu as pltpu
from jax.sharding import PartitionSpec as P

NT = (((1,), (1,)), ((), ()))
TN = (((0,), (0,)), ((), ()))
MESH = pl.DeviceIdType.MESH
UNROLLED_PEERS = 16
PANEL = 4


def pick_columns(folded, index, rank):
    width = folded.shape[1]
    count = index.shape[1]
    low = lax.rem(index, width)
    high = lax.div(index, width)
    rows = lax.broadcasted_iota(jnp.int16, (width, count), 0)
    one_hot = jnp.where(rows == low.astype(jnp.int16), jnp.bfloat16(1), jnp.bfloat16(0))
    products = jnp.dot(folded[...], one_hot, preferred_element_type=jnp.float32)
    picked = products[:rank]
    high = jnp.broadcast_to(high, (rank, count))
    for part in range(1, folded.shape[0] // rank):
        picked = jnp.where(high == part, products[part * rank : (part + 1) * rank], picked)
    return picked


def block_column(table_ref):
    table = jnp.concatenate([table_ref[tile] for tile in range(table_ref.shape[0])], axis=0)
    return jnp.concatenate(
        [table[:, peer : peer + 1] for peer in range(table.shape[1])], axis=0
    )


def inverse(matrix):
    order = matrix.shape[0]
    lanes = lax.broadcasted_iota(jnp.int32, (1, order), 1)
    rows = lax.broadcasted_iota(jnp.int32, (order, 1), 0)
    for first in range(0, order, PANEL):
        panel = [
            jnp.broadcast_to(matrix[:, k : k + 1], matrix.shape)
            for k in range(first, first + PANEL)
        ]
        for step in range(PANEL):
            k = first + step
            column = panel[step]
            pivot = 1.0 / column[k : k + 1, :]
            scaled = jnp.where(lanes == k, 1.0, matrix[k : k + 1, :]) * pivot
            own = rows == k
            matrix = jnp.where(
                own, scaled, jnp.where(lanes == k, 0.0, matrix) - column * scaled
            )
            for later in range(step + 1, PANEL):
                factor = panel[later][k : k + 1, :] * pivot
                panel[later] = jnp.where(own, factor, panel[later] - column * factor)
    return matrix


def kernel(
    n,
    tiles,
    slots,
    total_rows,
    total_samples,
    b_hbm,
    c_hbm,
    j_hbm,
    k_hbm,
    w_hbm,
    values_hbm,
    sample_hbm,
    count_hbm,
    out_ref,
    scales_ref,
    folded_b,
    folded_c,
    j_ref,
    k_ref,
    w_ref,
    values_ref,
    sample_ref,
    count_ref,
    c_out,
    c_in,
    b_weighted,
    values_out,
    values_in,
    spread_ref,
    picks_out,
    picks_in,
    gram_out,
    gram_in,
    share_out,
    share_in,
    sample_column,
    sums_out,
    sums_in,
    load_sems,
    c_send,
    c_recv,
    send_sems,
    recv_sems,
):
    me = lax.axis_index("row")
    rank, b_rows = b_hbm.shape
    c_rows = c_hbm.shape[1]
    width = folded_c.shape[1]
    per_peer = tiles * slots
    blocks = n * per_peer
    chunk = c_in.shape[2]
    half = n // 2
    side = me // half
    place = me % half

    def far(turn):
        return (1 - side) * half + (place + turn) % half

    def near(turn):
        return side * half + (place + turn) % half

    def loop(start, stop, body):
        if n <= UNROLLED_PEERS:
            for turn in range(start, stop):
                body(turn)
        else:
            lax.fori_loop(start, stop, lambda turn, carry: (body(turn), carry)[1], 0)

    def each_peer(body):
        loop(0, half, lambda turn: body(far(turn)))
        loop(1, half, lambda turn: body(near(turn)))

    def remote(peer, source, target, send, recv):
        return pltpu.make_async_remote_copy(
            src_ref=source,
            dst_ref=target,
            send_sem=send,
            recv_sem=recv,
            device_id={"row": peer},
            device_id_type=MESH,
        )

    def copy_c(peer, slot):
        return remote(peer, c_out.at[peer], c_in.at[slot], c_send.at[peer], c_recv.at[slot])

    def others(kind, target):
        region = target.at[pl.ds(0, n - 1)]
        return remote(near(1), region, region, send_sems.at[kind], recv_sems.at[kind])

    barrier = pltpu.get_barrier_semaphore()
    each_peer(
        lambda peer: pl.semaphore_signal(
            barrier, inc=1, device_id={"row": peer}, device_id_type=MESH
        )
    )

    def load_table(source, target, kind):
        return [
            pltpu.make_async_copy(
                source.at[:, pl.ds(part * width, width)],
                target.at[pl.ds(part * rank, rank)],
                load_sems.at[kind],
            )
            for part in range(source.shape[1] // width)
        ]

    load_c = load_table(c_hbm, folded_c, 0)
    load_b = load_table(b_hbm, folded_b, 1)
    load_k = pltpu.make_async_copy(k_hbm, k_ref, load_sems.at[2])
    load_j = pltpu.make_async_copy(j_hbm, j_ref, load_sems.at[3])
    load_w = pltpu.make_async_copy(w_hbm, w_ref, load_sems.at[4])
    load_values = pltpu.make_async_copy(values_hbm, values_ref, load_sems.at[5])
    load_sample = pltpu.make_async_copy(sample_hbm, sample_ref, load_sems.at[6])
    load_count = pltpu.make_async_copy(count_hbm, count_ref, load_sems.at[7])
    for load in [load_k, *load_c, load_count, load_values, load_sample, load_j, *load_b, load_w]:
        load.start()

    def pick_c(peer):
        return pick_columns(folded_c, k_ref[peer] - me * c_rows, rank).astype(jnp.bfloat16)

    load_k.wait()
    for load in load_c:
        load.wait()
    c_out[far(0)] = pick_c(far(0))
    load_count.wait()
    load_values.wait()
    lanes = lax.broadcasted_iota(jnp.int32, (blocks, 128), 1)
    counts = block_column(count_ref)
    live = lanes < counts
    masked = jnp.where(live, values_ref[...].astype(jnp.float32), 0.0).astype(jnp.bfloat16)
    values_out[...] = masked.reshape(values_out.shape)
    values_in[me] = values_out[me]
    live_local = jnp.sum(counts.astype(jnp.float32), axis=0, keepdims=True)
    pl.semaphore_wait(barrier, n - 1)
    copy_c(far(0), me).start()
    each_peer(
        lambda peer: remote(
            peer, values_out.at[peer], values_in.at[me], send_sems.at[0], recv_sems.at[0]
        ).start()
    )

    def send_c(peer):
        c_out[peer] = pick_c(peer)
        copy_c(peer, me).start()

    def send_far(turn, carry):
        send_c(far(turn))
        return carry

    def send_near(turn, carry):
        send_c(near(turn))
        return carry

    lax.fori_loop(1, half, send_far, 0)
    lax.fori_loop(1, half, send_near, 0)
    c_in[me] = pick_c(me)
    load_j.wait()
    load_w.wait()
    load_sample.wait()
    for load in load_b:
        load.wait()

    def pick_b(part, carry):
        picked = pick_columns(folded_b, j_ref[part] - me * b_rows, rank)
        b_weighted[part] = w_ref[part] * picked
        return carry

    lax.fori_loop(0, n, pick_b, 0)
    columns = lax.broadcasted_iota(jnp.int32, (blocks, chunk), 1)
    sample_column[...] = block_column(sample_ref)

    def add_chunk(part, carry):
        gram, picks = carry
        weights = w_ref[part]
        sketch = b_weighted[part] * c_in[part].astype(jnp.float32)
        top = sketch.astype(jnp.bfloat16)
        rest = (sketch - top.astype(jnp.float32)).astype(jnp.bfloat16)
        both = jnp.concatenate([top, rest], axis=0)
        gram = gram + lax.dot_general(both, both, NT, preferred_element_type=jnp.float32)
        weighted = (weights * sketch).astype(jnp.bfloat16)
        chosen = columns == sample_column[...] - part * chunk
        chosen = jnp.where(chosen, 1.0, 0.0).astype(jnp.bfloat16)
        picks = picks + lax.dot_general(
            chosen, weighted, NT, preferred_element_type=jnp.float32
        )
        return gram, picks

    def add_peer(part, carry):
        copy_c(part, part).wait_recv()
        return add_chunk(part, carry)

    carry = (
        jnp.zeros((2 * rank, 2 * rank), jnp.float32),
        jnp.zeros((blocks, rank), jnp.float32),
    )
    carry = add_chunk(me, carry)
    carry = lax.fori_loop(1, half, lambda turn, carry: add_peer(near(turn), carry), carry)

    others(0, values_in).wait_recv()
    arrived = values_in[...].astype(jnp.float32)
    rows_half = per_peer // 2
    tile_of = lax.broadcasted_iota(jnp.int32, (n * rows_half, 128), 0) % rows_half // slots
    for part in range(2):
        rows = arrived[:, part * rows_half : (part + 1) * rows_half, :].reshape(-1, 128)
        spread_ref[part] = jnp.concatenate(
            [jnp.where(tile_of == tile, rows, 0.0) for tile in range(tiles // 2)], axis=1
        ).astype(jnp.bfloat16)

    gram, picks = lax.fori_loop(
        0,
        half,
        lambda turn, carry: add_peer(side * turn + (1 - side) * (n - 1 - turn), carry),
        carry,
    )

    pair = gram[:rank] + gram[rank:]
    pair = (pair + pltpu.roll(pair, rank, 1)) / total_samples
    pair_rows = lax.broadcasted_iota(jnp.int32, pair.shape, 0)
    pair_lanes = lax.broadcasted_iota(jnp.int32, pair.shape, 1)
    ridge = 0.05 * live_local / total_rows
    pair = pair + jnp.where(pair_lanes % rank == pair_rows, ridge, 0.0)
    fold = rank // (n * gram_out.shape[1])
    if fold == 2:
        first_half = lax.broadcasted_iota(jnp.int32, (rank // 2, 2 * rank), 1) < rank
        pair = jnp.where(first_half, pair[: rank // 2], pair[rank // 2 :])
    piece = gram_out.shape[1]
    for part in range(n):
        gram_out[part] = pair[part * piece : (part + 1) * piece]
    gram_in[me] = gram_out[me]
    each_peer(
        lambda peer: remote(
            peer, gram_out.at[peer], gram_in.at[me], send_sems.at[1], recv_sems.at[1]
        ).start()
    )
    picks = picks.reshape(n, per_peer, rank)
    picks_out[...] = jnp.concatenate(
        [picks[:, :rows_half], picks[:, rows_half:]], axis=2
    ).astype(jnp.bfloat16)
    picks_in[me] = picks_out[me]
    each_peer(
        lambda peer: remote(
            peer, picks_out.at[peer], picks_in.at[me], send_sems.at[2], recv_sems.at[2]
        ).start()
    )
    others(1, gram_in).wait_recv()
    share_out[...] = jnp.sum(gram_in[...], axis=0)
    share_in[me] = share_out[...]
    each_peer(
        lambda peer: remote(
            peer, share_out, share_in.at[me], send_sems.at[3], recv_sems.at[3]
        ).start()
    )
    others(2, picks_in).wait_recv()
    arrived = picks_in[...].astype(jnp.float32).reshape(-1, 2 * rank).astype(jnp.bfloat16)
    gathered = jnp.concatenate(
        [
            lax.dot_general(arrived, spread_ref[part], TN, preferred_element_type=jnp.float32)[
                part * rank : (part + 1) * rank
            ]
            for part in range(2)
        ],
        axis=1,
    )
    others(3, share_in).wait_recv()
    total = jnp.concatenate([share_in[part] for part in range(n)], axis=0)
    if fold == 2:
        total = jnp.concatenate([total[:, :rank], total[:, rank:]], axis=0)
    else:
        total = total[:, :rank]
    inverted = inverse(total)
    update = jnp.dot(
        inverted,
        gathered,
        precision=lax.Precision.HIGHEST,
        preferred_element_type=jnp.float32,
    )
    gram_rows = lax.broadcasted_iota(jnp.int32, (rank, rank), 0)
    diagonal = gram_rows == lax.broadcasted_iota(jnp.int32, (rank, rank), 1)
    squares = jnp.sum(update * update, axis=1, keepdims=True)
    squares = jnp.sum(jnp.where(diagonal, squares, 0.0), axis=0, keepdims=True)
    sums_out[...] = jnp.concatenate([squares, jnp.zeros_like(squares)], axis=1)
    sums_in[me] = sums_out[...]
    each_peer(
        lambda peer: remote(
            peer, sums_out, sums_in.at[me], send_sems.at[4], recv_sems.at[4]
        ).start()
    )
    others(4, sums_in).wait_recv()
    sums = jnp.sum(sums_in[...], axis=0)
    scales = jnp.sqrt(sums[:, :rank] / total_rows + 1e-06)
    scales_ref[...] = scales
    scale_column = jnp.sum(jnp.where(diagonal, scales, 0.0), axis=1, keepdims=True)
    out_ref[...] = (update / scale_column).astype(out_ref.dtype)

    each_peer(lambda peer: copy_c(peer, me).wait_send())
    others(0, values_out).wait_send()
    others(1, gram_out).wait_send()
    others(2, picks_out).wait_send()
    others(3, share_in).wait_send()
    others(4, sums_in).wait_send()


def shards(
    factor_b, factor_c, sample_j, sample_k, sample_weight, block_values, block_sample, block_count
):
    rank, b_rows = factor_b.shape
    n, _, chunk = sample_k.shape
    _, _, tiles, slots, tile_rows = block_values.shape
    samples = sample_j.shape[0]
    per_peer = tiles * slots
    blocks = n * per_peer
    width = 512
    piece = max(rank // (2 * n), 1)
    bf16, f32, i32 = jnp.bfloat16, jnp.float32, jnp.int32
    hbm = pl.BlockSpec(memory_space=pltpu.HBM)
    vmem = pl.BlockSpec(memory_space=pltpu.VMEM)
    factor_new, scales = pl.pallas_call(
        functools.partial(kernel, n, tiles, slots, tiles * tile_rows * n, samples * n),
        out_shape=(
            pltpu.VMEM((rank, tiles * tile_rows), bf16),
            pltpu.VMEM((1, rank), f32),
        ),
        in_specs=[hbm] * 8,
        out_specs=(vmem, vmem),
        scratch_shapes=[
            pltpu.VMEM((b_rows // width * rank, width), bf16),
            pltpu.VMEM((factor_c.shape[1] // width * rank, width), bf16),
            pltpu.VMEM((n, 1, chunk), i32),
            pltpu.VMEM((n, 1, chunk), i32),
            pltpu.VMEM((n, 1, chunk), f32),
            pltpu.VMEM((blocks, tile_rows), bf16),
            pltpu.VMEM((tiles, slots, n), i32),
            pltpu.VMEM((tiles, slots, n), i32),
            pltpu.VMEM((n, rank, chunk), bf16),
            pltpu.VMEM((n, rank, chunk), bf16),
            pltpu.VMEM((n, rank, chunk), f32),
            pltpu.VMEM((n, per_peer, tile_rows), bf16),
            pltpu.VMEM((n, per_peer, tile_rows), bf16),
            pltpu.VMEM((2, blocks // 2, tiles // 2 * tile_rows), bf16),
            pltpu.VMEM((n, per_peer // 2, 2 * rank), bf16),
            pltpu.VMEM((n, per_peer // 2, 2 * rank), bf16),
            pltpu.VMEM((n, piece, 2 * rank), f32),
            pltpu.VMEM((n, piece, 2 * rank), f32),
            pltpu.VMEM((piece, 2 * rank), f32),
            pltpu.VMEM((n, piece, 2 * rank), f32),
            pltpu.VMEM((blocks, 1), i32),
            pltpu.VMEM((1, 2 * rank), f32),
            pltpu.VMEM((n, 1, 2 * rank), f32),
            pltpu.SemaphoreType.DMA((8,)),
            pltpu.SemaphoreType.DMA((n,)),
            pltpu.SemaphoreType.DMA((n,)),
            pltpu.SemaphoreType.DMA((5,)),
            pltpu.SemaphoreType.DMA((5,)),
        ],
        compiler_params=pltpu.CompilerParams(collective_id=0, has_side_effects=True),
    )(
        factor_b,
        factor_c,
        sample_j.reshape(n, 1, chunk),
        sample_k,
        sample_weight.reshape(n, 1, chunk),
        block_values.reshape(blocks, tile_rows),
        block_sample[0].transpose(1, 2, 0),
        block_count[0].transpose(1, 2, 0),
    )
    return factor_new, scales.reshape(rank)


def solution(mesh):
    in_specs = (
        P(None, ("groups", "row")),
        P(None, ("groups", "row")),
        P(("groups", "row")),
        P(None, ("groups", "row"), None),
        P(("groups", "row")),
        P(("groups", "row"), None, None, None, None),
        P(("groups", "row"), None, None, None),
        P(("groups", "row"), None, None, None),
    )
    out_specs = (P(None, ("groups", "row")), P("groups"))
    return jax.shard_map(shards, mesh=mesh, in_specs=in_specs, out_specs=out_specs, check_vma=False)
```

time: 59.7 us -> 49.4 us (0.83)
  Pallas kernels: 56.9 us -> 47.4 us
  local copies, waits for them, and re-layouts: 1.99 us -> 1.14 us
    pallas_call x1, Pallas kernels: 56.9 us -> 47.4 us  [shards(): pl.pallas_call(functools.partial(kernel, n, tiles, slots, tiles * tile_ro...]
    unnamed x4 -> x2, local copies, waits for them, and re-layouts: 1.99 us -> 1.14 us
where the time goes in v1:
time: 49.4 us; the launch traced here: 49.2 us
  Pallas kernels  47.4 us (96%)
  local copies, waits for them, and re-layouts  1.14 us (2%)
  between operations  0.64 us (1%)
    pallas_call x1, Pallas kernels, shards(): pl.pallas_call(functools.partial(kernel, n, tiles, slots, tiles * tile_ro...  47.4 us
    unnamed x2, local copies, waits for them, and re-layouts  1.14 us

profile of v1, /device:TPU:0, one launch (start us, length us, event | category | flops | bytes accessed | tf_op | source)
XLA Modules:
  0.0 49.2 jit_solution(1858606503859554499)
XLA Ops:
  0.6 47.4 %shard_map.95 = (bf16[64,512]{1,0:T(8,128)(2,1)S(1)}, f32[1,64]{1,0:T(1,128)S(1)}) custom-call(bf16[64,4096]{1,0:T(8,128)(2,1)} %b_hbm.1, bf16[64,4096]{1,0:T(8,128)(2,1)} %c_hbm.1, s32[16,1,512]{2,1,0:T(1,128)} %bitcast.12, s32[16,1,512]{2,1,0:T(1,128)} %k_hbm.1, f32[16,1,512]{2,1,0:T(1,128)} %bitcast.13, bf16[256,128]{1,0:T(8,128)(2,1)} %bitcast.11, ...), custom_call_target="tpu_custom_call" | custom-call | tf_op jit(solution)/shard_map/pallas_call | solution.py:380
  48.0 0.6 %copy.12 = bf16[64,512]{1,0:T(8,128)(2,1)} copy(bf16[64,512]{1,0:T(8,128)(2,1)S(1)} %get-tuple-element.6) | data formatting | bytes 131072
  48.7 0.5 %copy.13 = f32[64]{0:T(128)} copy(f32[64]{0:T(128)S(1)} %bitcast.10) | data formatting | bytes 512

commit v2 on v1

--- a/solution.py
+++ b/solution.py
@@ -97,8 +97,10 @@
     share_out,
     share_in,
     sample_column,
-    sums_out,
-    sums_in,
+    moment_out,
+    moment_in,
+    moments_out,
+    moments_in,
     load_sems,
     c_send,
     c_recv,
@@ -112,15 +114,27 @@
     per_peer = tiles * slots
     blocks = n * per_peer
     chunk = c_in.shape[2]
-    half = n // 2
-    side = me // half
-    place = me % half
-
-    def far(turn):
-        return (1 - side) * half + (place + turn) % half
-
-    def near(turn):
-        return side * half + (place + turn) % half
+    quarter = n // 4
+    own = me // quarter
+    place = me % quarter
+    side = own // 2
+    inner = (own + side) % 2
+
+    def member(frame, turn):
+        return (frame + side * (3 - 2 * frame)) * quarter + (place + turn) % quarter
+
+    def sibling(turn):
+        return own * quarter + (place + turn) % quarter
+
+    def send_turn(turn):
+        block = turn // quarter
+        first, last = (2 - block) // 2, block // 2
+        frame = first * (2 - 2 * inner) + (1 - first - last) * 3 + last * (1 + inner)
+        return member(frame, turn % quarter)
+
+    def late_turn(turn):
+        block = turn // quarter
+        return member((1 - block) * (3 - 3 * inner) + block * 2, turn % quarter)
 
     def loop(start, stop, body):
         if n <= UNROLLED_PEERS:
@@ -130,8 +144,9 @@
             lax.fori_loop(start, stop, lambda turn, carry: (body(turn), carry)[1], 0)
 
     def each_peer(body):
-        loop(0, half, lambda turn: body(far(turn)))
-        loop(1, half, lambda turn: body(near(turn)))
+        for frame in (3, 2, 1 - inner):
+            loop(0, quarter, lambda turn, frame=frame: body(member(frame, turn)))
+        loop(1, quarter, lambda turn: body(sibling(turn)))
 
     def remote(peer, source, target, send, recv):
         return pltpu.make_async_remote_copy(
@@ -148,7 +163,41 @@
 
     def others(kind, target):
         region = target.at[pl.ds(0, n - 1)]
-        return remote(near(1), region, region, send_sems.at[kind], recv_sems.at[kind])
+        return remote(sibling(1), region, region, send_sems.at[kind], recv_sems.at[kind])
+
+    def spread_out(source, target, kind):
+        each_peer(
+            lambda peer: remote(
+                peer, source.at[peer], target.at[me], send_sems.at[kind], recv_sems.at[kind]
+            ).start()
+        )
+
+    piece = gram_out.shape[1]
+    fold = rank // (n * piece)
+
+    def scatter(pair, source, target, kind):
+        if fold == 2:
+            upper = lax.broadcasted_iota(jnp.int32, (rank // 2, 2 * rank), 1) < rank
+            pair = jnp.where(upper, pair[: rank // 2], pair[rank // 2 :])
+        for part in range(n):
+            source[part] = pair[part * piece : (part + 1) * piece]
+        target[me] = source[me]
+        spread_out(source, target, kind)
+
+    def gather(arrived, source, target, kind):
+        source[...] = jnp.sum(arrived[...], axis=0)
+        target[me] = source[...]
+        each_peer(
+            lambda peer: remote(
+                peer, source, target.at[me], send_sems.at[kind], recv_sems.at[kind]
+            ).start()
+        )
+
+    def whole(arrived):
+        matrix = jnp.concatenate([arrived[part] for part in range(n)], axis=0)
+        if fold == 2:
+            return jnp.concatenate([matrix[:, :rank], matrix[:, rank:]], axis=0)
+        return matrix[:, :rank]
 
     barrier = pltpu.get_barrier_semaphore()
     each_peer(
@@ -184,7 +233,7 @@
     load_k.wait()
     for load in load_c:
         load.wait()
-    c_out[far(0)] = pick_c(far(0))
+    c_out[send_turn(0)] = pick_c(send_turn(0))
     load_count.wait()
     load_values.wait()
     lanes = lax.broadcasted_iota(jnp.int32, (blocks, 128), 1)
@@ -195,27 +244,23 @@
     values_in[me] = values_out[me]
     live_local = jnp.sum(counts.astype(jnp.float32), axis=0, keepdims=True)
     pl.semaphore_wait(barrier, n - 1)
-    copy_c(far(0), me).start()
-    each_peer(
-        lambda peer: remote(
-            peer, values_out.at[peer], values_in.at[me], send_sems.at[0], recv_sems.at[0]
-        ).start()
-    )
+    copy_c(send_turn(0), me).start()
 
     def send_c(peer):
         c_out[peer] = pick_c(peer)
         copy_c(peer, me).start()
 
     def send_far(turn, carry):
-        send_c(far(turn))
+        send_c(send_turn(turn))
         return carry
 
     def send_near(turn, carry):
-        send_c(near(turn))
+        send_c(sibling(turn))
         return carry
 
-    lax.fori_loop(1, half, send_far, 0)
-    lax.fori_loop(1, half, send_near, 0)
+    lax.fori_loop(1, 3 * quarter, send_far, 0)
+    lax.fori_loop(1, quarter, send_near, 0)
+    spread_out(values_out, values_in, 0)
     c_in[me] = pick_c(me)
     load_j.wait()
     load_w.wait()
@@ -257,11 +302,32 @@
         jnp.zeros((blocks, rank), jnp.float32),
     )
     carry = add_chunk(me, carry)
-    carry = lax.fori_loop(1, half, lambda turn, carry: add_peer(near(turn), carry), carry)
-
+    carry = lax.fori_loop(
+        0, quarter, lambda turn, carry: add_peer(member(1 + 2 * inner, turn), carry), carry
+    )
+    carry = lax.fori_loop(
+        1, quarter, lambda turn, carry: add_peer(sibling(turn), carry), carry
+    )
+    gram, picks = lax.fori_loop(
+        0, 2 * quarter, lambda turn, carry: add_peer(late_turn(turn), carry), carry
+    )
+
+    pair = gram[:rank] + gram[rank:]
+    pair = (pair + pltpu.roll(pair, rank, 1)) / total_samples
+    pair_rows = lax.broadcasted_iota(jnp.int32, pair.shape, 0)
+    pair_lanes = lax.broadcasted_iota(jnp.int32, pair.shape, 1)
+    ridge = 0.05 * live_local / total_rows
+    pair = pair + jnp.where(pair_lanes % rank == pair_rows, ridge, 0.0)
+    scatter(pair, gram_out, gram_in, 1)
+    rows_half = per_peer // 2
+    picks = picks.reshape(n, per_peer, rank)
+    picks_out[...] = jnp.concatenate(
+        [picks[:, :rows_half], picks[:, rows_half:]], axis=2
+    ).astype(jnp.bfloat16)
+    picks_in[me] = picks_out[me]
+    spread_out(picks_out, picks_in, 2)
     others(0, values_in).wait_recv()
     arrived = values_in[...].astype(jnp.float32)
-    rows_half = per_peer // 2
     tile_of = lax.broadcasted_iota(jnp.int32, (n * rows_half, 128), 0) % rows_half // slots
     for part in range(2):
         rows = arrived[:, part * rows_half : (part + 1) * rows_half, :].reshape(-1, 128)
@@ -269,50 +335,8 @@
             [jnp.where(tile_of == tile, rows, 0.0) for tile in range(tiles // 2)], axis=1
         ).astype(jnp.bfloat16)
 
-    gram, picks = lax.fori_loop(
-        0,
-        half,
-        lambda turn, carry: add_peer(side * turn + (1 - side) * (n - 1 - turn), carry),
-        carry,
-    )
-
-    pair = gram[:rank] + gram[rank:]
-    pair = (pair + pltpu.roll(pair, rank, 1)) / total_samples
-    pair_rows = lax.broadcasted_iota(jnp.int32, pair.shape, 0)
-    pair_lanes = lax.broadcasted_iota(jnp.int32, pair.shape, 1)
-    ridge = 0.05 * live_local / total_rows
-    pair = pair + jnp.where(pair_lanes % rank == pair_rows, ridge, 0.0)
-    fold = rank // (n * gram_out.shape[1])
-    if fold == 2:
-        first_half = lax.broadcasted_iota(jnp.int32, (rank // 2, 2 * rank), 1) < rank
-        pair = jnp.where(first_half, pair[: rank // 2], pair[rank // 2 :])
-    piece = gram_out.shape[1]
-    for part in range(n):
-        gram_out[part] = pair[part * piece : (part + 1) * piece]
-    gram_in[me] = gram_out[me]
-    each_peer(
-        lambda peer: remote(
-            peer, gram_out.at[peer], gram_in.at[me], send_sems.at[1], recv_sems.at[1]
-        ).start()
-    )
-    picks = picks.reshape(n, per_peer, rank)
-    picks_out[...] = jnp.concatenate(
-        [picks[:, :rows_half], picks[:, rows_half:]], axis=2
-    ).astype(jnp.bfloat16)
-    picks_in[me] = picks_out[me]
-    each_peer(
-        lambda peer: remote(
-            peer, picks_out.at[peer], picks_in.at[me], send_sems.at[2], recv_sems.at[2]
-        ).start()
-    )
     others(1, gram_in).wait_recv()
-    share_out[...] = jnp.sum(gram_in[...], axis=0)
-    share_in[me] = share_out[...]
-    each_peer(
-        lambda peer: remote(
-            peer, share_out, share_in.at[me], send_sems.at[3], recv_sems.at[3]
-        ).start()
-    )
+    gather(gram_in, share_out, share_in, 3)
     others(2, picks_in).wait_recv()
     arrived = picks_in[...].astype(jnp.float32).reshape(-1, 2 * rank).astype(jnp.bfloat16)
     gathered = jnp.concatenate(
@@ -324,12 +348,18 @@
         ],
         axis=1,
     )
+    moment = lax.dot_general(
+        gathered,
+        jnp.concatenate([gathered, gathered], axis=0),
+        NT,
+        precision=lax.Precision.HIGHEST,
+        preferred_element_type=jnp.float32,
+    )
+    scatter(moment, moment_out, moment_in, 4)
     others(3, share_in).wait_recv()
-    total = jnp.concatenate([share_in[part] for part in range(n)], axis=0)
-    if fold == 2:
-        total = jnp.concatenate([total[:, :rank], total[:, rank:]], axis=0)
-    else:
-        total = total[:, :rank]
+    others(4, moment_in).wait_recv()
+    gather(moment_in, moments_out, moments_in, 5)
+    total = whole(share_in)
     inverted = inverse(total)
     update = jnp.dot(
         inverted,
@@ -339,28 +369,25 @@
     )
     gram_rows = lax.broadcasted_iota(jnp.int32, (rank, rank), 0)
     diagonal = gram_rows == lax.broadcasted_iota(jnp.int32, (rank, rank), 1)
-    squares = jnp.sum(update * update, axis=1, keepdims=True)
-    squares = jnp.sum(jnp.where(diagonal, squares, 0.0), axis=0, keepdims=True)
-    sums_out[...] = jnp.concatenate([squares, jnp.zeros_like(squares)], axis=1)
-    sums_in[me] = sums_out[...]
-    each_peer(
-        lambda peer: remote(
-            peer, sums_out, sums_in.at[me], send_sems.at[4], recv_sems.at[4]
-        ).start()
-    )
-    others(4, sums_in).wait_recv()
-    sums = jnp.sum(sums_in[...], axis=0)
-    scales = jnp.sqrt(sums[:, :rank] / total_rows + 1e-06)
-    scales_ref[...] = scales
-    scale_column = jnp.sum(jnp.where(diagonal, scales, 0.0), axis=1, keepdims=True)
-    out_ref[...] = (update / scale_column).astype(out_ref.dtype)
+    others(5, moments_in).wait_recv()
+    solved = jnp.dot(
+        inverted,
+        whole(moments_in),
+        precision=lax.Precision.HIGHEST,
+        preferred_element_type=jnp.float32,
+    )
+    squares = jnp.sum(solved * inverted, axis=1, keepdims=True)
+    scales = jnp.sqrt(jnp.maximum(squares, 0.0) / total_rows + 1e-06)
+    out_ref[...] = (update / scales).astype(out_ref.dtype)
+    scales_ref[...] = jnp.sum(jnp.where(diagonal, scales, 0.0), axis=0, keepdims=True)
 
     each_peer(lambda peer: copy_c(peer, me).wait_send())
     others(0, values_out).wait_send()
     others(1, gram_out).wait_send()
     others(2, picks_out).wait_send()
     others(3, share_in).wait_send()
-    others(4, sums_in).wait_send()
+    others(4, moment_out).wait_send()
+    others(5, moments_in).wait_send()
 
 
 def shards(
@@ -407,13 +434,15 @@
             pltpu.VMEM((piece, 2 * rank), f32),
             pltpu.VMEM((n, piece, 2 * rank), f32),
             pltpu.VMEM((blocks, 1), i32),
-            pltpu.VMEM((1, 2 * rank), f32),
-            pltpu.VMEM((n, 1, 2 * rank), f32),
+            pltpu.VMEM((n, piece, 2 * rank), f32),
+            pltpu.VMEM((n, piece, 2 * rank), f32),
+            pltpu.VMEM((piece, 2 * rank), f32),
+            pltpu.VMEM((n, piece, 2 * rank), f32),
             pltpu.SemaphoreType.DMA((8,)),
             pltpu.SemaphoreType.DMA((n,)),
             pltpu.SemaphoreType.DMA((n,)),
-            pltpu.SemaphoreType.DMA((5,)),
-            pltpu.SemaphoreType.DMA((5,)),
+            pltpu.SemaphoreType.DMA((6,)),
+            pltpu.SemaphoreType.DMA((6,)),
         ],
         compiler_params=pltpu.CompilerParams(collective_id=0, has_side_effects=True),
     )(

time: 49.4 us -> 47.9 us (0.970)
  Pallas kernels: 47.4 us -> 46 us
    pallas_call x1, Pallas kernels: 47.4 us -> 46 us  [shards(): pl.pallas_call(functools.partial(kernel, n, tiles, slots, tiles * tile_ro...]
where the time goes in v2:
time: 47.9 us; the launch traced here: 47.8 us
  Pallas kernels  46 us (96%)
  local copies, waits for them, and re-layouts  1.14 us (2%)
  between operations  0.64 us (1%)
    pallas_call x1, Pallas kernels, shards(): pl.pallas_call(functools.partial(kernel, n, tiles, slots, tiles * tile_ro...  46 us
    unnamed x2, local copies, waits for them, and re-layouts  1.14 us

profile of v2, /device:TPU:0, one launch (start us, length us, event | category | flops | bytes accessed | tf_op | source)
XLA Modules:
  0.0 47.8 jit_solution(11819203319332247344)
XLA Ops:
  0.6 46.0 %shard_map.95 = (bf16[64,512]{1,0:T(8,128)(2,1)S(1)}, f32[1,64]{1,0:T(1,128)S(1)}) custom-call(bf16[64,4096]{1,0:T(8,128)(2,1)} %b_hbm.1, bf16[64,4096]{1,0:T(8,128)(2,1)} %c_hbm.1, s32[16,1,512]{2,1,0:T(1,128)} %bitcast.12, s32[16,1,512]{2,1,0:T(1,128)} %k_hbm.1, f32[16,1,512]{2,1,0:T(1,128)} %bitcast.13, bf16[256,128]{1,0:T(8,128)(2,1)} %bitcast.11, ...), custom_call_target="tpu_custom_call" | custom-call | tf_op jit(solution)/shard_map/pallas_call | solution.py:407
  46.6 0.6 %copy.12 = bf16[64,512]{1,0:T(8,128)(2,1)} copy(bf16[64,512]{1,0:T(8,128)(2,1)S(1)} %get-tuple-element.6) | data formatting | bytes 131072
  47.2 0.5 %copy.13 = f32[64]{0:T(128)} copy(f32[64]{0:T(128)S(1)} %bitcast.10) | data formatting | bytes 512

commit v3 on v2

--- a/solution.py
+++ b/solution.py
@@ -106,6 +106,7 @@
     c_recv,
     send_sems,
     recv_sems,
+    turn_sem,
 ):
     me = lax.axis_index("row")
     rank, b_rows = b_hbm.shape
@@ -134,7 +135,7 @@
 
     def late_turn(turn):
         block = turn // quarter
-        return member((1 - block) * (3 - 3 * inner) + block * 2, turn % quarter)
+        return member((1 - block) * (3 - 3 * inner) + block * 2, quarter - turn % quarter)
 
     def loop(start, stop, body):
         if n <= UNROLLED_PEERS:
@@ -260,7 +261,11 @@
 
     lax.fori_loop(1, 3 * quarter, send_far, 0)
     lax.fori_loop(1, quarter, send_near, 0)
-    spread_out(values_out, values_in, 0)
+
+    @pl.when(inner == 1)
+    def _():
+        spread_out(values_out, values_in, 0)
+
     c_in[me] = pick_c(me)
     load_j.wait()
     load_w.wait()
@@ -303,14 +308,37 @@
     )
     carry = add_chunk(me, carry)
     carry = lax.fori_loop(
-        0, quarter, lambda turn, carry: add_peer(member(1 + 2 * inner, turn), carry), carry
+        0, quarter, lambda turn, carry: add_peer(member(1 + 2 * inner, quarter - turn), carry), carry
     )
     carry = lax.fori_loop(
-        1, quarter, lambda turn, carry: add_peer(sibling(turn), carry), carry
-    )
-    gram, picks = lax.fori_loop(
-        0, 2 * quarter, lambda turn, carry: add_peer(late_turn(turn), carry), carry
-    )
+        1, quarter, lambda turn, carry: add_peer(sibling(quarter - turn), carry), carry
+    )
+
+    def add_late(turn, carry):
+        carry = add_peer(late_turn(turn), carry)
+
+        @pl.when((inner == 1) & (turn == 3 * quarter // 2 - 1))
+        def _():
+            pl.semaphore_signal(
+                turn_sem, inc=1, device_id={"row": member(0, 0)}, device_id_type=MESH
+            )
+
+        return carry
+
+    gram, picks = lax.fori_loop(0, 2 * quarter, add_late, carry)
+
+    @pl.when(inner == 0)
+    def _():
+        pl.semaphore_wait(turn_sem, 1)
+        spread_out(values_out, values_in, 0)
+
+    rows_half = per_peer // 2
+    picks = picks.reshape(n, per_peer, rank)
+    picks_out[...] = jnp.concatenate(
+        [picks[:, :rows_half], picks[:, rows_half:]], axis=2
+    ).astype(jnp.bfloat16)
+    picks_in[me] = picks_out[me]
+    spread_out(picks_out, picks_in, 2)
 
     pair = gram[:rank] + gram[rank:]
     pair = (pair + pltpu.roll(pair, rank, 1)) / total_samples
@@ -319,13 +347,7 @@
     ridge = 0.05 * live_local / total_rows
     pair = pair + jnp.where(pair_lanes % rank == pair_rows, ridge, 0.0)
     scatter(pair, gram_out, gram_in, 1)
-    rows_half = per_peer // 2
-    picks = picks.reshape(n, per_peer, rank)
-    picks_out[...] = jnp.concatenate(
-        [picks[:, :rows_half], picks[:, rows_half:]], axis=2
-    ).astype(jnp.bfloat16)
-    picks_in[me] = picks_out[me]
-    spread_out(picks_out, picks_in, 2)
+
     others(0, values_in).wait_recv()
     arrived = values_in[...].astype(jnp.float32)
     tile_of = lax.broadcasted_iota(jnp.int32, (n * rows_half, 128), 0) % rows_half // slots
@@ -335,8 +357,6 @@
             [jnp.where(tile_of == tile, rows, 0.0) for tile in range(tiles // 2)], axis=1
         ).astype(jnp.bfloat16)
 
-    others(1, gram_in).wait_recv()
-    gather(gram_in, share_out, share_in, 3)
     others(2, picks_in).wait_recv()
     arrived = picks_in[...].astype(jnp.float32).reshape(-1, 2 * rank).astype(jnp.bfloat16)
     gathered = jnp.concatenate(
@@ -356,9 +376,11 @@
         preferred_element_type=jnp.float32,
     )
     scatter(moment, moment_out, moment_in, 4)
-    others(3, share_in).wait_recv()
+    others(1, gram_in).wait_recv()
+    gather(gram_in, share_out, share_in, 3)
     others(4, moment_in).wait_recv()
     gather(moment_in, moments_out, moments_in, 5)
+    others(3, share_in).wait_recv()
     total = whole(share_in)
     inverted = inverse(total)
     update = jnp.dot(
@@ -443,6 +465,7 @@
             pltpu.SemaphoreType.DMA((n,)),
             pltpu.SemaphoreType.DMA((6,)),
             pltpu.SemaphoreType.DMA((6,)),
+            pltpu.SemaphoreType.REGULAR,
         ],
         compiler_params=pltpu.CompilerParams(collective_id=0, has_side_effects=True),
     )(

time: 47.9 us -> 46.8 us (0.977)
  Pallas kernels: 46 us -> 44.9 us
    pallas_call x1, Pallas kernels: 46 us -> 44.9 us  [shards(): pl.pallas_call(functools.partial(kernel, n, tiles, slots, tiles * tile_ro...]
where the time goes in v3:
time: 46.8 us; the launch traced here: 46.7 us
  Pallas kernels  44.9 us (96%)
  local copies, waits for them, and re-layouts  1.14 us (2%)
  between operations  0.64 us (1%)
    pallas_call x1, Pallas kernels, shards(): pl.pallas_call(functools.partial(kernel, n, tiles, slots, tiles * tile_ro...  44.9 us
    unnamed x2, local copies, waits for them, and re-layouts  1.14 us

profile of v3, /device:TPU:0, one launch (start us, length us, event | category | flops | bytes accessed | tf_op | source)
XLA Modules:
  0.0 46.7 jit_solution(6314451787910147210)
XLA Ops:
  0.6 44.9 %shard_map.95 = (bf16[64,512]{1,0:T(8,128)(2,1)S(1)}, f32[1,64]{1,0:T(1,128)S(1)}) custom-call(bf16[64,4096]{1,0:T(8,128)(2,1)} %b_hbm.1, bf16[64,4096]{1,0:T(8,128)(2,1)} %c_hbm.1, s32[16,1,512]{2,1,0:T(1,128)} %bitcast.12, s32[16,1,512]{2,1,0:T(1,128)} %k_hbm.1, f32[16,1,512]{2,1,0:T(1,128)} %bitcast.13, bf16[256,128]{1,0:T(8,128)(2,1)} %bitcast.11, ...), custom_call_target="tpu_custom_call" | custom-call | tf_op jit(solution)/shard_map/pallas_call | solution.py:429
  45.5 0.6 %copy.12 = bf16[64,512]{1,0:T(8,128)(2,1)} copy(bf16[64,512]{1,0:T(8,128)(2,1)S(1)} %get-tuple-element.6) | data formatting | bytes 131072
  46.1 0.5 %copy.13 = f32[64]{0:T(128)} copy(f32[64]{0:T(128)S(1)} %bitcast.10) | data formatting | bytes 512

commit v4 on v3

--- a/solution.py
+++ b/solution.py
@@ -7,6 +7,7 @@
 from jax.experimental.pallas import tpu as pltpu
 from jax.sharding import PartitionSpec as P
 
+NN = (((1,), (0,)), ((), ()))
 NT = (((1,), (1,)), ((), ()))
 TN = (((0,), (0,)), ((), ()))
 MESH = pl.DeviceIdType.MESH
@@ -33,6 +34,16 @@
     table = jnp.concatenate([table_ref[tile] for tile in range(table_ref.shape[0])], axis=0)
     return jnp.concatenate(
         [table[:, peer : peer + 1] for peer in range(table.shape[1])], axis=0
+    )
+
+
+def product(left, right, dimensions=NT):
+    return lax.dot_general(
+        left,
+        right,
+        dimensions,
+        precision=lax.Precision.HIGHEST,
+        preferred_element_type=jnp.float32,
     )
 
 
@@ -99,8 +110,6 @@
     sample_column,
     moment_out,
     moment_in,
-    moments_out,
-    moments_in,
     load_sems,
     c_send,
     c_recv,
@@ -173,6 +182,13 @@
             ).start()
         )
 
+    def broadcast(source, target, kind):
+        each_peer(
+            lambda peer: remote(
+                peer, source, target.at[me], send_sems.at[kind], recv_sems.at[kind]
+            ).start()
+        )
+
     piece = gram_out.shape[1]
     fold = rank // (n * piece)
 
@@ -188,11 +204,7 @@
     def gather(arrived, source, target, kind):
         source[...] = jnp.sum(arrived[...], axis=0)
         target[me] = source[...]
-        each_peer(
-            lambda peer: remote(
-                peer, source, target.at[me], send_sems.at[kind], recv_sems.at[kind]
-            ).start()
-        )
+        broadcast(source, target, kind)
 
     def whole(arrived):
         matrix = jnp.concatenate([arrived[part] for part in range(n)], axis=0)
@@ -368,39 +380,57 @@
         ],
         axis=1,
     )
-    moment = lax.dot_general(
-        gathered,
-        jnp.concatenate([gathered, gathered], axis=0),
-        NT,
-        precision=lax.Precision.HIGHEST,
-        preferred_element_type=jnp.float32,
-    )
-    scatter(moment, moment_out, moment_in, 4)
     others(1, gram_in).wait_recv()
     gather(gram_in, share_out, share_in, 3)
+
+    part = rank // 2
+    top = product(gathered[:part], jnp.concatenate([gathered] * 2, axis=0))
+    low = product(gathered[part:], jnp.concatenate([gathered[part:]] * 4, axis=0))
+    rows = lax.broadcasted_iota(jnp.int32, (part, 2 * rank), 0)
+    lanes = lax.broadcasted_iota(jnp.int32, (part, 2 * rank), 1)
+    across = lanes % rank
+    triangle = jnp.where(across >= rows, jnp.where(across == rows, top, 2.0 * top), 2.0 * low)
+    quarter_rows = part // 2
+    moment_out[:quarter_rows] = jnp.where(
+        lanes[:quarter_rows] < rank, triangle[:quarter_rows], triangle[quarter_rows:]
+    )
+    moment_out[quarter_rows:] = jnp.sum(
+        jnp.where(lanes == rows, low, 0.0), axis=0, keepdims=True
+    )
+    moment_in[me] = moment_out[...]
+    broadcast(moment_out, moment_in, 4)
+
+    others(3, share_in).wait_recv()
+    inverted = inverse(whole(share_in))
+    update = product(inverted, gathered, NN)
+    first = jnp.concatenate([inverted] * 2, axis=1)
+    second = jnp.concatenate([inverted[:, part:]] * 4, axis=1)
     others(4, moment_in).wait_recv()
-    gather(moment_in, moments_out, moments_in, 5)
-    others(3, share_in).wait_recv()
-    total = whole(share_in)
-    inverted = inverse(total)
-    update = jnp.dot(
-        inverted,
-        gathered,
-        precision=lax.Precision.HIGHEST,
-        preferred_element_type=jnp.float32,
-    )
-    gram_rows = lax.broadcasted_iota(jnp.int32, (rank, rank), 0)
-    diagonal = gram_rows == lax.broadcasted_iota(jnp.int32, (rank, rank), 1)
-    others(5, moments_in).wait_recv()
-    solved = jnp.dot(
-        inverted,
-        whole(moments_in),
-        precision=lax.Precision.HIGHEST,
-        preferred_element_type=jnp.float32,
-    )
-    squares = jnp.sum(solved * inverted, axis=1, keepdims=True)
+    moment = jnp.sum(moment_in[...], axis=0)
+    triangle, corner = moment[:quarter_rows], moment[quarter_rows:]
+    above = across >= rows
+    stacked = jnp.concatenate([triangle] * 2, axis=0)
+    stacked = jnp.where((lanes < rank) == (rows < quarter_rows), stacked, 0.0)
+    zeros = jnp.zeros_like(stacked)
+    stacked = jnp.concatenate(
+        [
+            jnp.concatenate([jnp.where(above, stacked, 0.0), zeros], axis=1),
+            jnp.concatenate([zeros, jnp.where(above, 0.0, stacked)], axis=1),
+        ],
+        axis=0,
+    )
+    solved = product(inverted, stacked, NN)
+    squares = jnp.sum(
+        solved[:, : 2 * rank] * first
+        + solved[:, 2 * rank :] * second
+        + corner * second * second,
+        axis=1,
+        keepdims=True,
+    )
     scales = jnp.sqrt(jnp.maximum(squares, 0.0) / total_rows + 1e-06)
     out_ref[...] = (update / scales).astype(out_ref.dtype)
+    diagonal = lax.broadcasted_iota(jnp.int32, (rank, rank), 0)
+    diagonal = diagonal == lax.broadcasted_iota(jnp.int32, (rank, rank), 1)
     scales_ref[...] = jnp.sum(jnp.where(diagonal, scales, 0.0), axis=0, keepdims=True)
 
     each_peer(lambda peer: copy_c(peer, me).wait_send())
@@ -408,8 +438,7 @@
     others(1, gram_out).wait_send()
     others(2, picks_out).wait_send()
     others(3, share_in).wait_send()
-    others(4, moment_out).wait_send()
-    others(5, moments_in).wait_send()
+    others(4, moment_in).wait_send()
 
 
 def shards(
@@ -456,15 +485,13 @@
             pltpu.VMEM((piece, 2 * rank), f32),
             pltpu.VMEM((n, piece, 2 * rank), f32),
             pltpu.VMEM((blocks, 1), i32),
-            pltpu.VMEM((n, piece, 2 * rank), f32),
-            pltpu.VMEM((n, piece, 2 * rank), f32),
-            pltpu.VMEM((piece, 2 * rank), f32),
-            pltpu.VMEM((n, piece, 2 * rank), f32),
+            pltpu.VMEM((rank // 4 + 1, 2 * rank), f32),
+            pltpu.VMEM((n, rank // 4 + 1, 2 * rank), f32),
             pltpu.SemaphoreType.DMA((8,)),
             pltpu.SemaphoreType.DMA((n,)),
             pltpu.SemaphoreType.DMA((n,)),
-            pltpu.SemaphoreType.DMA((6,)),
-            pltpu.SemaphoreType.DMA((6,)),
+            pltpu.SemaphoreType.DMA((5,)),
+            pltpu.SemaphoreType.DMA((5,)),
             pltpu.SemaphoreType.REGULAR,
         ],
         compiler_params=pltpu.CompilerParams(collective_id=0, has_side_effects=True),

time: 46.8 us -> 45 us (0.962)
  Pallas kernels: 44.9 us -> 43 us
    pallas_call x1, Pallas kernels: 44.9 us -> 43 us  [shards(): pl.pallas_call(functools.partial(kernel, n, tiles, slots, tiles * tile_ro...]
where the time goes in v4:
time: 45 us; the launch traced here: 44.8 us
  Pallas kernels  43 us (96%)
  local copies, waits for them, and re-layouts  1.14 us (3%)
  between operations  0.64 us (1%)
    pallas_call x1, Pallas kernels, shards(): pl.pallas_call(functools.partial(kernel, n, tiles, slots, tiles * tile_ro...  43 us
    unnamed x2, local copies, waits for them, and re-layouts  1.14 us

profile of v4, /device:TPU:0, one launch (start us, length us, event | category | flops | bytes accessed | tf_op | source)
XLA Modules:
  0.0 44.8 jit_solution(16998819190270700541)
XLA Ops:
  0.6 43.0 %shard_map.95 = (bf16[64,512]{1,0:T(8,128)(2,1)S(1)}, f32[1,64]{1,0:T(1,128)S(1)}) custom-call(bf16[64,4096]{1,0:T(8,128)(2,1)} %b_hbm.1, bf16[64,4096]{1,0:T(8,128)(2,1)} %c_hbm.1, s32[16,1,512]{2,1,0:T(1,128)} %bitcast.12, s32[16,1,512]{2,1,0:T(1,128)} %k_hbm.1, f32[16,1,512]{2,1,0:T(1,128)} %bitcast.13, bf16[256,128]{1,0:T(8,128)(2,1)} %bitcast.11, ...), custom_call_target="tpu_custom_call" | custom-call | tf_op jit(solution)/shard_map/pallas_call | solution.py:458
  43.7 0.6 %copy.12 = bf16[64,512]{1,0:T(8,128)(2,1)} copy(bf16[64,512]{1,0:T(8,128)(2,1)S(1)} %get-tuple-element.6) | data formatting | bytes 131072
  44.3 0.5 %copy.13 = f32[64]{0:T(128)} copy(f32[64]{0:T(128)S(1)} %bitcast.10) | data formatting | bytes 512

commit v5 on v4

--- a/solution.py
+++ b/solution.py
@@ -12,7 +12,7 @@
 TN = (((0,), (0,)), ((), ()))
 MESH = pl.DeviceIdType.MESH
 UNROLLED_PEERS = 16
-PANEL = 4
+PANEL = 8
 
 
 def pick_columns(folded, index, rank):
@@ -49,26 +49,32 @@
 
 def inverse(matrix):
     order = matrix.shape[0]
-    lanes = lax.broadcasted_iota(jnp.int32, (1, order), 1)
-    rows = lax.broadcasted_iota(jnp.int32, (order, 1), 0)
+    lanes = lax.broadcasted_iota(jnp.int32, (8, order), 1)
+    rows = lax.broadcasted_iota(jnp.int32, (8, order), 0)
+    blocks = [matrix[first : first + 8] for first in range(0, order, 8)]
     for first in range(0, order, PANEL):
         panel = [
-            jnp.broadcast_to(matrix[:, k : k + 1], matrix.shape)
+            [jnp.broadcast_to(block[:, k : k + 1], block.shape) for block in blocks]
             for k in range(first, first + PANEL)
         ]
         for step in range(PANEL):
             k = first + step
+            home, place = divmod(k, 8)
             column = panel[step]
-            pivot = 1.0 / column[k : k + 1, :]
-            scaled = jnp.where(lanes == k, 1.0, matrix[k : k + 1, :]) * pivot
-            own = rows == k
-            matrix = jnp.where(
-                own, scaled, jnp.where(lanes == k, 0.0, matrix) - column * scaled
-            )
+            pivot = 1.0 / column[home][place : place + 1]
+            scaled = jnp.where(lanes[:1] == k, 1.0, blocks[home][place : place + 1]) * pivot
+            blocks = [
+                jnp.where(lanes == k, 0.0, block) - part * scaled
+                for block, part in zip(blocks, column)
+            ]
+            blocks[home] = jnp.where(rows == place, scaled, blocks[home])
             for later in range(step + 1, PANEL):
-                factor = panel[later][k : k + 1, :] * pivot
-                panel[later] = jnp.where(own, factor, panel[later] - column * factor)
-    return matrix
+                factor = panel[later][home][place : place + 1] * pivot
+                panel[later] = [
+                    block - part * factor for block, part in zip(panel[later], column)
+                ]
+                panel[later][home] = jnp.where(rows == place, factor, panel[later][home])
+    return jnp.concatenate(blocks, axis=0)
 
 
 def kernel(
@@ -139,7 +145,10 @@
     def send_turn(turn):
         block = turn // quarter
         first, last = (2 - block) // 2, block // 2
-        frame = first * (2 - 2 * inner) + (1 - first - last) * 3 + last * (1 + inner)
+        middle = 1 - first - last
+        swap = inner * ((quarter - turn % quarter) // quarter) * (middle - first)
+        first, middle = first + swap, middle - swap
+        frame = first * (2 - 2 * inner) + middle * 3 + last * (1 + inner)
         return member(frame, turn % quarter)
 
     def late_turn(turn):

time: 45 us -> 43.4 us (0.964)
  Pallas kernels: 43 us -> 41.4 us
    pallas_call x1, Pallas kernels: 43 us -> 41.4 us  [shards(): pl.pallas_call(functools.partial(kernel, n, tiles, slots, tiles * tile_ro...]
where the time goes in v5:
time: 43.4 us; the launch traced here: 43.2 us
  Pallas kernels  41.4 us (95%)
  local copies, waits for them, and re-layouts  1.14 us (3%)
  between operations  0.64 us (1%)
    pallas_call x1, Pallas kernels, shards(): pl.pallas_call(functools.partial(kernel, n, tiles, slots, tiles * tile_ro...  41.4 us
    unnamed x2, local copies, waits for them, and re-layouts  1.14 us

profile of v5, /device:TPU:0, one launch (start us, length us, event | category | flops | bytes accessed | tf_op | source)
XLA Modules:
  0.0 43.2 jit_solution(8127338425815091076)
XLA Ops:
  0.6 41.4 %shard_map.95 = (bf16[64,512]{1,0:T(8,128)(2,1)S(1)}, f32[1,64]{1,0:T(1,128)S(1)}) custom-call(bf16[64,4096]{1,0:T(8,128)(2,1)} %b_hbm.1, bf16[64,4096]{1,0:T(8,128)(2,1)} %c_hbm.1, s32[16,1,512]{2,1,0:T(1,128)} %bitcast.12, s32[16,1,512]{2,1,0:T(1,128)} %k_hbm.1, f32[16,1,512]{2,1,0:T(1,128)} %bitcast.13, bf16[256,128]{1,0:T(8,128)(2,1)} %bitcast.11, ...), custom_call_target="tpu_custom_call" | custom-call | tf_op jit(solution)/shard_map/pallas_call | solution.py:467
  42.0 0.6 %copy.12 = bf16[64,512]{1,0:T(8,128)(2,1)} copy(bf16[64,512]{1,0:T(8,128)(2,1)S(1)} %get-tuple-element.6) | data formatting | bytes 131072
  42.7 0.5 %copy.13 = f32[64]{0:T(128)} copy(f32[64]{0:T(128)S(1)} %bitcast.10) | data formatting | bytes 512

commit v6 on v5

--- a/solution.py
+++ b/solution.py
@@ -91,8 +91,8 @@
     values_hbm,
     sample_hbm,
     count_hbm,
-    out_ref,
-    scales_ref,
+    update_ref,
+    squares_ref,
     folded_b,
     folded_c,
     j_ref,
@@ -117,9 +117,8 @@
     moment_out,
     moment_in,
     load_sems,
-    c_send,
     c_recv,
-    send_sems,
+    send_sem,
     recv_sems,
     turn_sem,
 ):
@@ -178,23 +177,23 @@
         )
 
     def copy_c(peer, slot):
-        return remote(peer, c_out.at[peer], c_in.at[slot], c_send.at[peer], c_recv.at[slot])
+        return remote(peer, c_out.at[peer], c_in.at[slot], send_sem, c_recv.at[slot])
 
     def others(kind, target):
         region = target.at[pl.ds(0, n - 1)]
-        return remote(sibling(1), region, region, send_sems.at[kind], recv_sems.at[kind])
+        return remote(sibling(1), region, region, send_sem, recv_sems.at[kind])
 
     def spread_out(source, target, kind):
         each_peer(
             lambda peer: remote(
-                peer, source.at[peer], target.at[me], send_sems.at[kind], recv_sems.at[kind]
+                peer, source.at[peer], target.at[me], send_sem, recv_sems.at[kind]
             ).start()
         )
 
     def broadcast(source, target, kind):
         each_peer(
             lambda peer: remote(
-                peer, source, target.at[me], send_sems.at[kind], recv_sems.at[kind]
+                peer, source, target.at[me], send_sem, recv_sems.at[kind]
             ).start()
         )
 
@@ -238,26 +237,30 @@
             for part in range(source.shape[1] // width)
         ]
 
-    load_c = load_table(c_hbm, folded_c, 0)
-    load_b = load_table(b_hbm, folded_b, 1)
-    load_k = pltpu.make_async_copy(k_hbm, k_ref, load_sems.at[2])
-    load_j = pltpu.make_async_copy(j_hbm, j_ref, load_sems.at[3])
-    load_w = pltpu.make_async_copy(w_hbm, w_ref, load_sems.at[4])
-    load_values = pltpu.make_async_copy(values_hbm, values_ref, load_sems.at[5])
-    load_sample = pltpu.make_async_copy(sample_hbm, sample_ref, load_sems.at[6])
-    load_count = pltpu.make_async_copy(count_hbm, count_ref, load_sems.at[7])
-    for load in [load_k, *load_c, load_count, load_values, load_sample, load_j, *load_b, load_w]:
-        load.start()
+    def load(source, target, kind):
+        return [pltpu.make_async_copy(source, target, load_sems.at[kind])]
+
+    loads = [
+        load(k_hbm, k_ref, 0) + load_table(c_hbm, folded_c, 0),
+        load(count_hbm, count_ref, 1)
+        + load(values_hbm, values_ref, 1)
+        + load(sample_hbm, sample_ref, 1),
+        load(j_hbm, j_ref, 2) + load(w_hbm, w_ref, 2) + load_table(b_hbm, folded_b, 2),
+    ]
+    for copies in loads:
+        for copy in copies:
+            copy.start()
+
+    def loaded(kind):
+        for copy in loads[kind]:
+            copy.wait()
 
     def pick_c(peer):
         return pick_columns(folded_c, k_ref[peer] - me * c_rows, rank).astype(jnp.bfloat16)
 
-    load_k.wait()
-    for load in load_c:
-        load.wait()
+    loaded(0)
     c_out[send_turn(0)] = pick_c(send_turn(0))
-    load_count.wait()
-    load_values.wait()
+    loaded(1)
     lanes = lax.broadcasted_iota(jnp.int32, (blocks, 128), 1)
     counts = block_column(count_ref)
     live = lanes < counts
@@ -288,11 +291,7 @@
         spread_out(values_out, values_in, 0)
 
     c_in[me] = pick_c(me)
-    load_j.wait()
-    load_w.wait()
-    load_sample.wait()
-    for load in load_b:
-        load.wait()
+    loaded(2)
 
     def pick_b(part, carry):
         picked = pick_columns(folded_b, j_ref[part] - me * b_rows, rank)
@@ -353,6 +352,14 @@
         pl.semaphore_wait(turn_sem, 1)
         spread_out(values_out, values_in, 0)
 
+    pair = gram[:rank] + gram[rank:]
+    pair = (pair + pltpu.roll(pair, rank, 1)) / total_samples
+    pair_rows = lax.broadcasted_iota(jnp.int32, pair.shape, 0)
+    pair_lanes = lax.broadcasted_iota(jnp.int32, pair.shape, 1)
+    ridge = 0.05 * live_local / total_rows
+    pair = pair + jnp.where(pair_lanes % rank == pair_rows, ridge, 0.0)
+    scatter(pair, gram_out, gram_in, 1)
+
     rows_half = per_peer // 2
     picks = picks.reshape(n, per_peer, rank)
     picks_out[...] = jnp.concatenate(
@@ -360,14 +367,6 @@
     ).astype(jnp.bfloat16)
     picks_in[me] = picks_out[me]
     spread_out(picks_out, picks_in, 2)
-
-    pair = gram[:rank] + gram[rank:]
-    pair = (pair + pltpu.roll(pair, rank, 1)) / total_samples
-    pair_rows = lax.broadcasted_iota(jnp.int32, pair.shape, 0)
-    pair_lanes = lax.broadcasted_iota(jnp.int32, pair.shape, 1)
-    ridge = 0.05 * live_local / total_rows
-    pair = pair + jnp.where(pair_lanes % rank == pair_rows, ridge, 0.0)
-    scatter(pair, gram_out, gram_in, 1)
 
     others(0, values_in).wait_recv()
     arrived = values_in[...].astype(jnp.float32)
@@ -378,6 +377,8 @@
             [jnp.where(tile_of == tile, rows, 0.0) for tile in range(tiles // 2)], axis=1
         ).astype(jnp.bfloat16)
 
+    others(1, gram_in).wait_recv()
+    gather(gram_in, share_out, share_in, 3)
     others(2, picks_in).wait_recv()
     arrived = picks_in[...].astype(jnp.float32).reshape(-1, 2 * rank).astype(jnp.bfloat16)
     gathered = jnp.concatenate(
@@ -389,9 +390,6 @@
         ],
         axis=1,
     )
-    others(1, gram_in).wait_recv()
-    gather(gram_in, share_out, share_in, 3)
-
     part = rank // 2
     top = product(gathered[:part], jnp.concatenate([gathered] * 2, axis=0))
     low = product(gathered[part:], jnp.concatenate([gathered[part:]] * 4, axis=0))
@@ -411,7 +409,6 @@
 
     others(3, share_in).wait_recv()
     inverted = inverse(whole(share_in))
-    update = product(inverted, gathered, NN)
     first = jnp.concatenate([inverted] * 2, axis=1)
     second = jnp.concatenate([inverted[:, part:]] * 4, axis=1)
     others(4, moment_in).wait_recv()
@@ -428,7 +425,8 @@
         ],
         axis=0,
     )
-    solved = product(inverted, stacked, NN)
+    both = product(inverted, jnp.concatenate([stacked, gathered], axis=1), NN)
+    solved, update_ref[...] = both[:, : 4 * rank], both[:, 4 * rank :]
     squares = jnp.sum(
         solved[:, : 2 * rank] * first
         + solved[:, 2 * rank :] * second
@@ -436,18 +434,10 @@
         axis=1,
         keepdims=True,
     )
-    scales = jnp.sqrt(jnp.maximum(squares, 0.0) / total_rows + 1e-06)
-    out_ref[...] = (update / scales).astype(out_ref.dtype)
-    diagonal = lax.broadcasted_iota(jnp.int32, (rank, rank), 0)
-    diagonal = diagonal == lax.broadcasted_iota(jnp.int32, (rank, rank), 1)
-    scales_ref[...] = jnp.sum(jnp.where(diagonal, scales, 0.0), axis=0, keepdims=True)
-
-    each_peer(lambda peer: copy_c(peer, me).wait_send())
-    others(0, values_out).wait_send()
-    others(1, gram_out).wait_send()
-    others(2, picks_out).wait_send()
-    others(3, share_in).wait_send()
-    others(4, moment_in).wait_send()
+    squares_ref[...] = squares
+
+    for sent in (c_out, values_out, gram_out, picks_out, share_in, moment_in):
+        others(0, sent).wait_send()
 
 
 def shards(
@@ -464,11 +454,12 @@
     bf16, f32, i32 = jnp.bfloat16, jnp.float32, jnp.int32
     hbm = pl.BlockSpec(memory_space=pltpu.HBM)
     vmem = pl.BlockSpec(memory_space=pltpu.VMEM)
-    factor_new, scales = pl.pallas_call(
-        functools.partial(kernel, n, tiles, slots, tiles * tile_rows * n, samples * n),
+    total_rows = tiles * tile_rows * n
+    update, squares = pl.pallas_call(
+        functools.partial(kernel, n, tiles, slots, total_rows, samples * n),
         out_shape=(
-            pltpu.VMEM((rank, tiles * tile_rows), bf16),
-            pltpu.VMEM((1, rank), f32),
+            pltpu.VMEM((rank, tiles * tile_rows), f32),
+            pltpu.VMEM((rank, 1), f32),
         ),
         in_specs=[hbm] * 8,
         out_specs=(vmem, vmem),
@@ -496,10 +487,9 @@
             pltpu.VMEM((blocks, 1), i32),
             pltpu.VMEM((rank // 4 + 1, 2 * rank), f32),
             pltpu.VMEM((n, rank // 4 + 1, 2 * rank), f32),
-            pltpu.SemaphoreType.DMA((8,)),
+            pltpu.SemaphoreType.DMA((3,)),
             pltpu.SemaphoreType.DMA((n,)),
-            pltpu.SemaphoreType.DMA((n,)),
-            pltpu.SemaphoreType.DMA((5,)),
+            pltpu.SemaphoreType.DMA,
             pltpu.SemaphoreType.DMA((5,)),
             pltpu.SemaphoreType.REGULAR,
         ],
@@ -514,7 +504,8 @@
         block_sample[0].transpose(1, 2, 0),
         block_count[0].transpose(1, 2, 0),
     )
-    return factor_new, scales.reshape(rank)
+    scales = jnp.sqrt(jnp.maximum(squares, 0.0) / total_rows + 1e-06)
+    return (update / scales).astype(bf16), scales.reshape(rank)
 
 
 def solution(mesh):

time: 43.4 us -> 42.1 us (0.970)
  local copies, waits for them, and re-layouts: 1.14 us -> 0.01 us
  Pallas kernels: 41.4 us -> 40.4 us
  other arithmetic: 0 us -> 0.83 us
    unnamed x2, local copies, waits for them, and re-layouts: 1.14 us -> 0.01 us
    pallas_call x1, Pallas kernels: 41.4 us -> 40.4 us  [shards(): pl.pallas_call(functools.partial(kernel, n, tiles, slots, total_rows, sam...]
    convert_element_type x0 -> x1, other arithmetic: none -> 0.71 us  [shards(): return ((update / scales).astype(bf16), scales.reshape(rank))]
where the time goes in v6:
time: 42.1 us; the launch traced here: 41.9 us
  Pallas kernels  40.4 us (96%)
  other arithmetic  0.83 us (2%)
  between operations  0.65 us (2%)
    pallas_call x1, Pallas kernels, shards(): pl.pallas_call(functools.partial(kernel, n, tiles, slots, total_rows, sam...  40.4 us

profile of v6, /device:TPU:0, one launch (start us, length us, event | category | flops | bytes accessed | tf_op | source)
XLA Modules:
  0.0 41.9 jit_solution(6550379845214554342)
XLA Ops:
  0.6 40.4 %shard_map.95 = (f32[64,512]{1,0:T(8,128)S(1)}, f32[64,1]{1,0:T(8,128)S(1)}) custom-call(bf16[64,4096]{1,0:T(8,128)(2,1)} %b_hbm.1, bf16[64,4096]{1,0:T(8,128)(2,1)} %c_hbm.1, s32[16,1,512]{2,1,0:T(1,128)} %bitcast.10, s32[16,1,512]{2,1,0:T(1,128)} %k_hbm.1, f32[16,1,512]{2,1,0:T(1,128)} %bitcast.11, bf16[256,128]{1,0:T(8,128)(2,1)} %bitcast.9, ...), custom_call_target="tpu_custom_call" | custom-call | tf_op jit(solution)/shard_map/pallas_call | solution.py:458
  41.1 0.1 sqrt_reduce_fusion
  41.2 0.0 copy-start
  41.2 0.7 %divide_convert_fusion = bf16[64,512]{1,0:T(8,128)(2,1)} fusion(f32[64,512]{1,0:T(8,128)S(1)} %get-tuple-element.4, f32[64]{0:T(128)S(1)} %sqrt_reduce_fusion), kind=kLoop, calls=%fused_computation | loop fusion | flops 65536 | bytes 196864 | tf_op jit(solution)/shard_map/convert_element_type | solution.py:508
  41.9 0.0 copy-done
Async XLA Ops:
  41.2 0.7 %copy-start = (f32[64]{0:T(128)}, f32[64]{0:T(128)S(1)}, u32[]{:S(2)}) copy-start(f32[64]{0:T(128)S(1)} %sqrt_reduce_fusion) | copy-start | bytes 772

commit v7 on v6

--- a/solution.py
+++ b/solution.py
@@ -7,7 +7,6 @@
 from jax.experimental.pallas import tpu as pltpu
 from jax.sharding import PartitionSpec as P
 
-NN = (((1,), (0,)), ((), ()))
 NT = (((1,), (1,)), ((), ()))
 TN = (((0,), (0,)), ((), ()))
 MESH = pl.DeviceIdType.MESH
@@ -37,14 +36,15 @@
     )
 
 
-def product(left, right, dimensions=NT):
-    return lax.dot_general(
-        left,
-        right,
-        dimensions,
-        precision=lax.Precision.HIGHEST,
-        preferred_element_type=jnp.float32,
-    )
+def product(left, right):
+    return jnp.dot(
+        left, right, precision=lax.Precision.HIGHEST, preferred_element_type=jnp.float32
+    )
+
+
+def halves(matrix):
+    top = matrix.astype(jnp.bfloat16)
+    return top, (matrix - top.astype(jnp.float32)).astype(jnp.bfloat16)
 
 
 def inverse(matrix):
@@ -306,9 +306,7 @@
         gram, picks = carry
         weights = w_ref[part]
         sketch = b_weighted[part] * c_in[part].astype(jnp.float32)
-        top = sketch.astype(jnp.bfloat16)
-        rest = (sketch - top.astype(jnp.float32)).astype(jnp.bfloat16)
-        both = jnp.concatenate([top, rest], axis=0)
+        both = jnp.concatenate(halves(sketch), axis=0)
         gram = gram + lax.dot_general(both, both, NT, preferred_element_type=jnp.float32)
         weighted = (weights * sketch).astype(jnp.bfloat16)
         chosen = columns == sample_column[...] - part * chunk
@@ -391,8 +389,14 @@
         axis=1,
     )
     part = rank // 2
-    top = product(gathered[:part], jnp.concatenate([gathered] * 2, axis=0))
-    low = product(gathered[part:], jnp.concatenate([gathered[part:]] * 4, axis=0))
+    split = halves(gathered)
+    columns = [jnp.concatenate([x] * 2 + [x[part:]] * 4, axis=0) for x in split]
+    split = jnp.concatenate(split, axis=0)
+    moments = sum(
+        lax.dot_general(split, x, NT, preferred_element_type=jnp.float32) for x in columns
+    )
+    moments = moments[:rank] + moments[rank:]
+    top, low = moments[:part, : 2 * rank], moments[part:, 2 * rank :]
     rows = lax.broadcasted_iota(jnp.int32, (part, 2 * rank), 0)
     lanes = lax.broadcasted_iota(jnp.int32, (part, 2 * rank), 1)
     across = lanes % rank
@@ -425,7 +429,7 @@
         ],
         axis=0,
     )
-    both = product(inverted, jnp.concatenate([stacked, gathered], axis=1), NN)
+    both = product(inverted, jnp.concatenate([stacked, gathered], axis=1))
     solved, update_ref[...] = both[:, : 4 * rank], both[:, 4 * rank :]
     squares = jnp.sum(
         solved[:, : 2 * rank] * first

time: 42.1 us -> 42 us (level)
  no operation moved by 1% of the time
where the time goes in v7:
time: 42 us; the launch traced here: 41.8 us
  Pallas kernels  40.4 us (96%)
  other arithmetic  0.83 us (2%)
  between operations  0.65 us (2%)
    pallas_call x1, Pallas kernels, shards(): pl.pallas_call(functools.partial(kernel, n, tiles, slots, total_rows, sam...  40.4 us

profile of v7, /device:TPU:0, one launch (start us, length us, event | category | flops | bytes accessed | tf_op | source)
XLA Modules:
  0.0 41.8 jit_solution(18327218926011238973)
XLA Ops:
  0.6 40.4 %shard_map.95 = (f32[64,512]{1,0:T(8,128)S(1)}, f32[64,1]{1,0:T(8,128)S(1)}) custom-call(bf16[64,4096]{1,0:T(8,128)(2,1)} %b_hbm.1, bf16[64,4096]{1,0:T(8,128)(2,1)} %c_hbm.1, s32[16,1,512]{2,1,0:T(1,128)} %bitcast.10, s32[16,1,512]{2,1,0:T(1,128)} %k_hbm.1, f32[16,1,512]{2,1,0:T(1,128)} %bitcast.11, bf16[256,128]{1,0:T(8,128)(2,1)} %bitcast.9, ...), custom_call_target="tpu_custom_call" | custom-call | tf_op jit(solution)/shard_map/pallas_call | solution.py:462
  41.0 0.1 sqrt_reduce_fusion
  41.1 0.0 copy-start
  41.1 0.7 %divide_convert_fusion = bf16[64,512]{1,0:T(8,128)(2,1)} fusion(f32[64,512]{1,0:T(8,128)S(1)} %get-tuple-element.4, f32[64]{0:T(128)S(1)} %sqrt_reduce_fusion), kind=kLoop, calls=%fused_computation | loop fusion | flops 65536 | bytes 196864 | tf_op jit(solution)/shard_map/convert_element_type | solution.py:512
  41.8 0.0 copy-done
Async XLA Ops:
  41.1 0.7 %copy-start = (f32[64]{0:T(128)}, f32[64]{0:T(128)S(1)}, u32[]{:S(2)}) copy-start(f32[64]{0:T(128)S(1)} %sqrt_reduce_fusion) | copy-start | bytes 772

commit v8 on v7

--- a/solution.py
+++ b/solution.py
@@ -162,9 +162,10 @@
             lax.fori_loop(start, stop, lambda turn, carry: (body(turn), carry)[1], 0)
 
     def each_peer(body):
-        for frame in (3, 2, 1 - inner):
-            loop(0, quarter, lambda turn, frame=frame: body(member(frame, turn)))
+        for frame in (3, 1 - inner):
+            loop(0, quarter, lambda turn, frame=frame: body(member(frame, turn - place + quarter)))
         loop(1, quarter, lambda turn: body(sibling(turn)))
+        loop(0, quarter, lambda turn: body(member(2, turn - place + quarter)))
 
     def remote(peer, source, target, send, recv):
         return pltpu.make_async_remote_copy(

time: 42 us -> 41.8 us (level)
  no operation moved by 1% of the time
where the time goes in v8:
time: 41.8 us; the launch traced here: 41.6 us
  Pallas kernels  40.1 us (96%)
  other arithmetic  0.83 us (2%)
  between operations  0.65 us (2%)
    pallas_call x1, Pallas kernels, shards(): pl.pallas_call(functools.partial(kernel, n, tiles, slots, total_rows, sam...  40.1 us

profile of v8, /device:TPU:0, one launch (start us, length us, event | category | flops | bytes accessed | tf_op | source)
XLA Modules:
  0.0 41.6 jit_solution(8711521440290382684)
XLA Ops:
  0.6 40.1 %shard_map.95 = (f32[64,512]{1,0:T(8,128)S(1)}, f32[64,1]{1,0:T(8,128)S(1)}) custom-call(bf16[64,4096]{1,0:T(8,128)(2,1)} %b_hbm.1, bf16[64,4096]{1,0:T(8,128)(2,1)} %c_hbm.1, s32[16,1,512]{2,1,0:T(1,128)} %bitcast.10, s32[16,1,512]{2,1,0:T(1,128)} %k_hbm.1, f32[16,1,512]{2,1,0:T(1,128)} %bitcast.11, bf16[256,128]{1,0:T(8,128)(2,1)} %bitcast.9, ...), custom_call_target="tpu_custom_call" | custom-call | tf_op jit(solution)/shard_map/pallas_call | solution.py:463
  40.8 0.1 sqrt_reduce_fusion
  40.9 0.0 copy-start
  40.9 0.7 %divide_convert_fusion = bf16[64,512]{1,0:T(8,128)(2,1)} fusion(f32[64,512]{1,0:T(8,128)S(1)} %get-tuple-element.4, f32[64]{0:T(128)S(1)} %sqrt_reduce_fusion), kind=kLoop, calls=%fused_computation | loop fusion | flops 65536 | bytes 196864 | tf_op jit(solution)/shard_map/convert_element_type | solution.py:513
  41.6 0.0 copy-done
Async XLA Ops:
  40.9 0.7 %copy-start = (f32[64]{0:T(128)}, f32[64]{0:T(128)S(1)}, u32[]{:S(2)}) copy-start(f32[64]{0:T(128)S(1)} %sqrt_reduce_fusion) | copy-start | bytes 772

commit v9 on v8

--- a/solution.py
+++ b/solution.py
@@ -11,7 +11,6 @@
 TN = (((0,), (0,)), ((), ()))
 MESH = pl.DeviceIdType.MESH
 UNROLLED_PEERS = 16
-PANEL = 8
 
 
 def pick_columns(folded, index, rank):
@@ -52,28 +51,47 @@
     lanes = lax.broadcasted_iota(jnp.int32, (8, order), 1)
     rows = lax.broadcasted_iota(jnp.int32, (8, order), 0)
     blocks = [matrix[first : first + 8] for first in range(0, order, 8)]
-    for first in range(0, order, PANEL):
-        panel = [
-            [jnp.broadcast_to(block[:, k : k + 1], block.shape) for block in blocks]
-            for k in range(first, first + PANEL)
+
+    def spread(block, first):
+        return [
+            jnp.broadcast_to(block[:, k : k + 1], block.shape) for k in range(first, first + 8)
         ]
-        for step in range(PANEL):
+
+    own = spread(blocks[0], 0)
+    for home in range(len(blocks)):
+        first = 8 * home
+        last = home + 1 == len(blocks)
+        spreads = [
+            own if place == home else spread(block, first) for place, block in enumerate(blocks)
+        ]
+        panel = [list(column) for column in zip(*spreads)]
+        if not last:
+            ahead = spread(blocks[home], first + 8)
+            following = spread(blocks[home + 1], first + 8)
+        for step in range(8):
             k = first + step
-            home, place = divmod(k, 8)
             column = panel[step]
-            pivot = 1.0 / column[home][place : place + 1]
-            scaled = jnp.where(lanes[:1] == k, 1.0, blocks[home][place : place + 1]) * pivot
+            pivot = 1.0 / own[step][step : step + 1]
+            scaled = jnp.where(lanes[:1] == k, 1.0, blocks[home][step : step + 1]) * pivot
             blocks = [
                 jnp.where(lanes == k, 0.0, block) - part * scaled
                 for block, part in zip(blocks, column)
             ]
-            blocks[home] = jnp.where(rows == place, scaled, blocks[home])
-            for later in range(step + 1, PANEL):
-                factor = panel[later][home][place : place + 1] * pivot
+            blocks[home] = jnp.where(rows == step, scaled, blocks[home])
+            for later in range(step + 1, 8):
+                factor = own[later][step : step + 1] * pivot
+                own[later] = own[later] - own[step] * factor
                 panel[later] = [
                     block - part * factor for block, part in zip(panel[later], column)
                 ]
-                panel[later][home] = jnp.where(rows == place, factor, panel[later][home])
+                panel[later][home] = jnp.where(rows == step, factor, panel[later][home])
+            if not last:
+                for later in range(8):
+                    factor = ahead[later][step : step + 1] * pivot
+                    ahead[later] = ahead[later] - own[step] * factor
+                    following[later] = following[later] - column[home + 1] * factor
+        if not last:
+            own = following
     return jnp.concatenate(blocks, axis=0)
 
 
@@ -145,7 +163,7 @@
         block = turn // quarter
         first, last = (2 - block) // 2, block // 2
         middle = 1 - first - last
-        swap = inner * ((quarter - turn % quarter) // quarter) * (middle - first)
+        swap = inner * ((quarter + 1 - turn % quarter) // quarter) * (middle - first)
         first, middle = first + swap, middle - swap
         frame = first * (2 - 2 * inner) + middle * 3 + last * (1 + inner)
         return member(frame, turn % quarter)

time: 41.8 us -> 41.4 us (level)
  no operation moved by 1% of the time
where the time goes in v9:
time: 41.4 us; the launch traced here: 41.2 us
  Pallas kernels  39.7 us (96%)
  other arithmetic  0.83 us (2%)
  between operations  0.65 us (2%)
    pallas_call x1, Pallas kernels, shards(): pl.pallas_call(functools.partial(kernel, n, tiles, slots, total_rows, sam...  39.7 us

profile of v9, /device:TPU:0, one launch (start us, length us, event | category | flops | bytes accessed | tf_op | source)
XLA Modules:
  0.0 41.2 jit_solution(17513236254426398011)
XLA Ops:
  0.6 39.7 %shard_map.95 = (f32[64,512]{1,0:T(8,128)S(1)}, f32[64,1]{1,0:T(8,128)S(1)}) custom-call(bf16[64,4096]{1,0:T(8,128)(2,1)} %b_hbm.1, bf16[64,4096]{1,0:T(8,128)(2,1)} %c_hbm.1, s32[16,1,512]{2,1,0:T(1,128)} %bitcast.10, s32[16,1,512]{2,1,0:T(1,128)} %k_hbm.1, f32[16,1,512]{2,1,0:T(1,128)} %bitcast.11, bf16[256,128]{1,0:T(8,128)(2,1)} %bitcast.9, ...), custom_call_target="tpu_custom_call" | custom-call | tf_op jit(solution)/shard_map/pallas_call | solution.py:481
  40.3 0.1 sqrt_reduce_fusion
  40.5 0.0 copy-start
  40.5 0.7 %divide_convert_fusion = bf16[64,512]{1,0:T(8,128)(2,1)} fusion(f32[64,512]{1,0:T(8,128)S(1)} %get-tuple-element.4, f32[64]{0:T(128)S(1)} %sqrt_reduce_fusion), kind=kLoop, calls=%fused_computation | loop fusion | flops 65536 | bytes 196864 | tf_op jit(solution)/shard_map/convert_element_type | solution.py:531
  41.2 0.0 copy-done
Async XLA Ops:
  40.5 0.7 %copy-start = (f32[64]{0:T(128)}, f32[64]{0:T(128)S(1)}, u32[]{:S(2)}) copy-start(f32[64]{0:T(128)S(1)} %sqrt_reduce_fusion) | copy-start | bytes 772
